TPU v7x, 32 devices: a whole 2x2x4 slice. The times are simulated.
32 devices in a mesh: tm: 4 (over y, core), lat: 8 (over z, x).
Axes of the slice: x: 2, y: 2, z: 4, core: 2. Of those that a mesh axis runs over, the one named last changes fastest.
Arguments:
- trajectory: float32 [4, 32, 64, 2048], P('tm', 'lat'), may hold values from -6 to 6
- diffusivity: float32 [4, 32, 64, 2048], P('tm', 'lat'), may hold values from 0.02 to 0.24
- adjoint_end: bfloat16 [32, 64, 2048], P('lat'), may hold values from -6 to 6
- obs_jac: bfloat16 [3072, 128, 128], P(('tm', 'lat')), may hold values from -0.5 to 0.5
- obs_value: float32 [3072, 128], P(('tm', 'lat')), may hold values from -6 to 6
- obs_weight: float32 [3072, 128], P(('tm', 'lat')), may hold values from 0.3 to 3
- obs_valid: int32 [3072, 128], P(('tm', 'lat')), may hold values 0 or 1
- obs_owner: int32 [3072, 1], P(('tm', 'lat')), may hold values from 0 to 31; in each aligned block of 96 rows (0 to 95, 96 to 191, ...) at most 6 rows name the same one
- obs_tile: int32 [3072], P(('tm', 'lat')), may hold values from 0 to 4095
Outputs:
- adjoint: float32 [4, 32, 64, 2048], P('tm', 'lat')
Inputs may be any that keep to these rules, and one draw needn't show every extreme that they name: `obs_owner`: among the 96 blocks of one device, no owner is named more than 6 times, a bound that some block reaches.
All inputs are finite; a program needn't handle non-finite values. No bound on the sum of `obs_valid` on one device may be relied on, other than what follows from the above.
Results may differ from a plain program's by a relative error of at most 0.0024.
Values may be sent and summed in bfloat16 or wider, within the bound.
No kernel may reach another device: no remote copies, remote signals or barrier semaphores. Data moves between devices by JAX's collectives and lax.ppermute only.
A program may use at most 128 MiB of HBM per device.

v0:
```python
import jax
import jax.numpy as jnp
from jax import lax
from jax.sharding import PartitionSpec as P

TW = 2
SUB = 2


def extended(block, sides, width):
    for axis, dim in sides:
        count = lax.axis_size(axis)
        forward = [(i, i + 1) for i in range(count - 1)]
        backward = [(target, source) for source, target in forward]
        low = lax.ppermute(
            lax.slice_in_dim(block, block.shape[dim] - width, None, axis=dim), axis, forward
        )
        high = lax.ppermute(lax.slice_in_dim(block, 0, width, axis=dim), axis, backward)
        block = jnp.concatenate([low, block, high], axis=dim)
    return block


def passed_along(block, axis, distance):
    devices = range(lax.axis_size(axis))
    route = [(i - distance, i) for i in devices if i - distance in devices]
    return lax.ppermute(block, axis, route)


def block_terms(jac, state, value, weight):
    jac_f = jac.astype(jnp.float32)
    pred = jnp.einsum("bct,bt->bc", jac_f, state, precision=lax.Precision.HIGHEST)
    resid = weight * (value - pred)
    return jnp.einsum("bct,bc->bt", jac_f, resid, precision=lax.Precision.HIGHEST)


def wrap_pad(values, width, axis_pos):
    last = values.shape[axis_pos]
    left = lax.slice_in_dim(values, last - width, last, axis=axis_pos)
    right = lax.slice_in_dim(values, 0, width, axis=axis_pos)
    return jnp.concatenate([left, values, right], axis=axis_pos)


def lon_edges_one(weighted):
    return wrap_pad(weighted, 1, 2)


def propagate(field, coeffs):
    for step in range(SUB):
        weighted = coeffs * field
        padded = extended(weighted, (("lat", 0),), 1)
        sides = lon_edges_one(weighted)
        field = (
            field + padded[2:] + padded[:-2] + sides[:, :, 2:] + sides[:, :, :-2] - 4.0 * weighted
        )
    return field


def per_device(
    trajectory,
    diffusivity,
    adjoint_end,
    obs_jac,
    obs_value,
    obs_weight,
    obs_valid,
    obs_owner,
    obs_tile,
):
    traj = trajectory[0]
    lat_dev, levels, nlon = traj.shape
    per_row = nlon // TW
    tile_len = levels * TW
    devices = lax.axis_size("tm") * lax.axis_size("lat")
    blocks = obs_owner.shape[0]
    slots = max(2, 2 * blocks // devices)
    count = devices * slots
    states = (
        traj.reshape(lat_dev, levels, per_row, TW)
        .transpose(0, 2, 1, 3)
        .reshape(lat_dev * per_row, tile_len)
    )
    target = obs_owner[:, 0]
    onehot = (target[:, None] == jnp.arange(devices, dtype=jnp.int32)[None, :]).astype(jnp.int32)
    rank = jnp.sum(onehot * (jnp.cumsum(onehot, 0) - 1), 1)
    slot = target * slots + rank

    def place(values):
        buffer = jnp.zeros((count,) + values.shape[1:], values.dtype).at[slot].set(values)
        return buffer.reshape((devices, slots) + values.shape[1:])

    weights = obs_weight * obs_valid.astype(jnp.float32)
    tile_ids = lax.all_to_all(
        place(obs_tile), ("tm", "lat"), split_axis=0, concat_axis=0, tiled=True
    ).reshape(count)
    found = states[tile_ids].reshape(devices, slots, tile_len)
    returned = lax.all_to_all(
        found, ("tm", "lat"), split_axis=0, concat_axis=0, tiled=True
    ).reshape(count, tile_len)
    mine = returned[slot]
    terms = block_terms(obs_jac, mine, obs_value, weights)
    received = lax.all_to_all(
        place(terms), ("tm", "lat"), split_axis=0, concat_axis=0, tiled=True
    ).reshape(count, tile_len)
    forcing = jnp.zeros((lat_dev * per_row, tile_len), jnp.float32).at[tile_ids].add(received)
    forcing = (
        forcing.reshape(lat_dev, per_row, levels, TW)
        .transpose(0, 2, 1, 3)
        .reshape(lat_dev, levels, nlon)
    )
    section_count = lax.axis_size("tm")
    coeff_own = diffusivity[0]
    is_last = lax.axis_index("tm") == section_count - 1

    def advance(step, current):
        handed = passed_along(current.astype(jnp.bfloat16), "tm", -1)
        incoming = jnp.where(is_last, adjoint_end, handed).astype(jnp.float32)
        return forcing + propagate(incoming, coeff_own)

    result = lax.fori_loop(0, section_count, advance, forcing)
    return result[None]


def solution(mesh):
    in_specs = (
        P("tm", "lat", None, None),
        P("tm", "lat", None, None),
        P("lat", None, None),
        P(("tm", "lat"), None, None),
        P(("tm", "lat"), None),
        P(("tm", "lat"), None),
        P(("tm", "lat"), None),
        P(("tm", "lat"), None),
        P(("tm", "lat")),
    )
    out_specs = P("tm", "lat", None, None)
    return jax.shard_map(
        per_device, mesh=mesh, in_specs=in_specs, out_specs=out_specs, check_vma=False
    )
```

profile of v0, /device:TPU:12, one launch (start us, length us, event | category | flops | bytes accessed | tf_op | source)
XLA Modules:
  0.0 394.2 jit_solution(13552812722194581030)
XLA Ops:
  4.3 6.0 %all-to-all-start = ((s32[32,1,6]{2,1,0:T(1,128)}), s32[32,1,6]{2,1,0:T(1,128)S(1)}, u32[]{:S(2)}, u32[]{:S(2)}) async-start(s32[32,1,6]{2,1,0:T(1,128)} %bitcast.3), calls=%async_computation | async-start | bytes 32768 | tf_op jit(solution)/shard_map/all_to_all | solution.py:92
  10.3 3.8 copy.25
  14.0 6.7 %copy.26 = f32[4,1024,64,2]{1,0,3,2:T(4,128)} copy(f32[4,1024,64,2]{2,3,1,0:T(2,128)} %bitcast.41) | data formatting | bytes 4194304 | tf_op jit(solution)/shard_map/transpose | solution.py:79
  20.7 4.6 %copy.36 = f32[16,8,4,1024]{3,1,2,0:T(8,128)} copy(f32[16,8,4,1024]{3,2,1,0:T(4,128)} %bitcast.42) | data formatting | bytes 4194304
  25.3 2.9 copy.27
  29.5 2.3 gather_fusion
  32.5 5.8 %all-to-all-start.1 = ((f32[32,6,128]{2,1,0:T(8,128)}), f32[32,6,128]{2,1,0:T(8,128)S(1)}, u32[]{:S(2)}, u32[]{:S(2)}) async-start(f32[32,6,128]{2,1,0:T(8,128)} %reshape.60), calls=%async_computation.1 | async-start | bytes 262144 | tf_op jit(solution)/shard_map/all_to_all | solution.py:96
  38.4 5.9 %all-to-all-done.1 = f32[32,6,128]{2,1,0:T(8,128)S(1)} async-done(((f32[32,6,128]{2,1,0:T(8,128)}), f32[32,6,128]{2,1,0:T(8,128)S(1)}, u32[]{:S(2)}, u32[]{:S(2)}) %all-to-all-start.1) | async-done | bytes 98336 | tf_op jit(solution)/shard_map/all_to_all | solution.py:96
  44.9 5.0 %fusion.23 = f32[96,1,128]{2,1,0:T(1,128)S(1)} fusion(f32[96,128,1]{1,2,0:T(1,128)S(1)} %bitcast.45, bf16[96,128,128]{2,1,0:T(8,128)(2,1)S(1)} %copy-done), kind=kOutput, calls=%fused_computation.47 | convolution fusion | flops 18874368 | bytes 3244032 | tf_op jit(solution)/shard_map/bct,bt->bc/dot_general | solution.py:31
  49.9 2.5 fusion.24
  54.0 4.4 %all-to-all-start.2 = ((f32[32,6,128]{2,1,0:T(8,128)}), f32[32,6,128]{2,1,0:T(8,128)S(1)}, u32[]{:S(2)}, u32[]{:S(2)}) async-start(f32[32,6,128]{2,1,0:T(8,128)} %reshape.62), calls=%async_computation.2 | async-start | bytes 262144 | tf_op jit(solution)/shard_map/all_to_all | solution.py:101
  58.4 6.0 %all-to-all-done.2 = f32[32,6,128]{2,1,0:T(8,128)S(1)} async-done(((f32[32,6,128]{2,1,0:T(8,128)}), f32[32,6,128]{2,1,0:T(8,128)S(1)}, u32[]{:S(2)}, u32[]{:S(2)}) %all-to-all-start.2) | async-done | bytes 98336 | tf_op jit(solution)/shard_map/all_to_all | solution.py:101
  64.4 2.8 scatter_custom_fusion.2
  67.2 2.9 copy.28
  70.1 3.6 reshape.64
  73.8 6.7 %copy.29 = f32[4,64,1024,2]{1,3,2,0:T(2,128)} copy(f32[4,64,1024,2]{2,0,3,1:T(4,128)} %bitcast.43) | data formatting | bytes 4194304 | tf_op jit(solution)/shard_map/transpose | solution.py:107
  80.4 3.8 copy.30
  84.2 3.1 copy.38
  87.3 306.7 %while.10 = (s32[]{:T(128)}, f32[4,64,2048]{2,1,0:T(8,128)}, pred[]{:T(512)}, bf16[4,64,2048]{2,1,0:T(8,128)(2,1)}, f32[4,64,2048]{2,1,0:T(8,128)}, /*index=5*/f32[4,64,2048]{2,1,0:T(8,128)}, s32[]{:T(128)}) while((s32[]{:T(128)}, f32[4,64,2048]{2,1,0:T(8,128)}, pred[]{:T(512)}, bf16[4,64,2048]{2,1,0:T(8,128)(2,1)}, f32[4,64,2048]{2,1,0:T(8,128)}, ...), condition=%wide.region_6.7_spmd, body=%wide.region_5.6_spmd.sunk | while | flops 20971520 | bytes 85998040 | solution.py:119
  89.2 2.5 collective-permute-start
  91.8 12.3 %collective-permute-done = bf16[4,64,2048]{2,1,0:T(8,128)(2,1)S(1)} collective-permute-done((bf16[4,64,2048]{2,1,0:T(8,128)(2,1)S(1)}, bf16[4,64,2048]{2,1,0:T(8,128)(2,1)S(1)}, u32[]{:S(2)}, u32[]{:S(2)}) %collective-permute-start) | collective-permute-done | bytes 1048608 | tf_op jit(solution)/shard_map/while/body/eval_jaxpr/ppermute | solution.py:26
  104.7 3.5 collective-permute-start.1
  108.2 3.2 collective-permute-start.2
  111.6 9.0 %collective-permute-done.1 = f32[1,64,2048]{2,1,0:T(8,128)S(1)} collective-permute-done((f32[1,64,2048]{2,1,0:T(8,128)S(1)}, f32[1,64,2048]{2,1,0:T(8,128)S(1)}, u32[]{:S(2)}, u32[]{:S(2)}) %collective-permute-start.1) | collective-permute-done | bytes 524320 | tf_op jit(solution)/shard_map/while/body/eval_jaxpr/ppermute | solution.py:15
  120.5 1.9 collective-permute-done.2
  125.7 2.5 collective-permute-start.3
  128.2 4.9 %collective-permute-start.4 = (f32[1,64,2048]{2,1,0:T(8,128)}, f32[1,64,2048]{2,1,0:T(8,128)}, u32[]{:S(2)}, u32[]{:S(2)}) collective-permute-start(f32[1,64,2048]{2,1,0:T(8,128)} %get-tuple-element.128), channel_id=1, source_target_pairs={{1,0},{2,1},{3,2},{4,3},{5,4},{6,5},{7,6},{9,8},{10,9},{11,10},{12... | collective-permute-start | bytes 1572872 | tf_op jit(solution)/shard_map/while/body/eval_jaxpr/ppermute | solution.py:18
  134.2 4.6 %collective-permute-done.3 = f32[1,64,2048]{2,1,0:T(8,128)} collective-permute-done((f32[1,64,2048]{2,1,0:T(8,128)}, f32[1,64,2048]{2,1,0:T(8,128)}, u32[]{:S(2)}, u32[]{:S(2)}) %collective-permute-start.3) | collective-permute-done | bytes 524320 | tf_op jit(solution)/shard_map/while/body/eval_jaxpr/ppermute | solution.py:15
  138.8 9.7 %collective-permute-done.4 = f32[1,64,2048]{2,1,0:T(8,128)} collective-permute-done((f32[1,64,2048]{2,1,0:T(8,128)}, f32[1,64,2048]{2,1,0:T(8,128)}, u32[]{:S(2)}, u32[]{:S(2)}) %collective-permute-start.4) | collective-permute-done | bytes 524320 | tf_op jit(solution)/shard_map/while/body/eval_jaxpr/ppermute | solution.py:18
  148.4 11.1 %fusion.40 = f32[4,64,2048]{2,1,0:T(8,128)} fusion(f32[4,64,2048]{2,1,0:T(8,128)} %get-tuple-element.148, f32[4,64,2048]{2,1,0:T(8,128)} %copy-done.2, f32[4,64,1]{2,1,0:T(8,128)S(1)} %get-tuple-element.125, f32[4,64,1]{2,1,0:T(8,128)S(1)} %get-tuple-element.126, f32[1,64,2048]{2,1,0:T(8,128)} %collective-permute-done.3, ...), kind=kLoop, calls=%fused_computation.14.clone.1 | loop fusion | flops 12058624 | bytes 12587009 | tf_op jit(solution)/shard_map/while/body/eval_jaxpr/add | solution.py:117
  161.4 5.0 %collective-permute-start = (bf16[4,64,2048]{2,1,0:T(8,128)(2,1)S(1)}, bf16[4,64,2048]{2,1,0:T(8,128)(2,1)S(1)}, u32[]{:S(2)}, u32[]{:S(2)}) collective-permute-start(bf16[4,64,2048]{2,1,0:T(8,128)(2,1)S(1)} %convert_element_type.38), channel_id=1, source_target_pairs={{8,0},{16,8},{24,16},{9,1},{17,9},{25,17},{10,2},{18,10},{26,18},{... | collective-permute-start | bytes 3145736 | tf_op jit(solution)/shard_map/while/body/eval_jaxpr/ppermute | solution.py:26
  166.4 12.3 %collective-permute-done = bf16[4,64,2048]{2,1,0:T(8,128)(2,1)S(1)} collective-permute-done((bf16[4,64,2048]{2,1,0:T(8,128)(2,1)S(1)}, bf16[4,64,2048]{2,1,0:T(8,128)(2,1)S(1)}, u32[]{:S(2)}, u32[]{:S(2)}) %collective-permute-start) | collective-permute-done | bytes 1048608 | tf_op jit(solution)/shard_map/while/body/eval_jaxpr/ppermute | solution.py:26
  179.3 1.9 collective-permute-start.1
  181.2 4.8 %collective-permute-start.2 = (f32[1,64,2048]{2,1,0:T(8,128)S(1)}, f32[1,64,2048]{2,1,0:T(8,128)S(1)}, u32[]{:S(2)}, u32[]{:S(2)}) collective-permute-start(f32[1,64,2048]{2,1,0:T(8,128)S(1)} %get-tuple-element.124), channel_id=1, source_target_pairs={{1,0},{2,1},{3,2},{4,3},{5,4},{6,5},{7,6},{9,8},{10,9},{11,10},{12... | collective-permute-start | bytes 1572872 | tf_op jit(solution)/shard_map/while/body/eval_jaxpr/ppermute | solution.py:18
  186.2 5.2 %collective-permute-done.1 = f32[1,64,2048]{2,1,0:T(8,128)S(1)} collective-permute-done((f32[1,64,2048]{2,1,0:T(8,128)S(1)}, f32[1,64,2048]{2,1,0:T(8,128)S(1)}, u32[]{:S(2)}, u32[]{:S(2)}) %collective-permute-start.1) | collective-permute-done | bytes 524320 | tf_op jit(solution)/shard_map/while/body/eval_jaxpr/ppermute | solution.py:15
  191.4 15.9 %collective-permute-done.2 = f32[1,64,2048]{2,1,0:T(8,128)S(1)} collective-permute-done((f32[1,64,2048]{2,1,0:T(8,128)S(1)}, f32[1,64,2048]{2,1,0:T(8,128)S(1)}, u32[]{:S(2)}, u32[]{:S(2)}) %collective-permute-start.2) | collective-permute-done | bytes 524320 | tf_op jit(solution)/shard_map/while/body/eval_jaxpr/ppermute | solution.py:18
  210.5 1.9 collective-permute-start.3
  212.5 4.8 %collective-permute-start.4 = (f32[1,64,2048]{2,1,0:T(8,128)}, f32[1,64,2048]{2,1,0:T(8,128)}, u32[]{:S(2)}, u32[]{:S(2)}) collective-permute-start(f32[1,64,2048]{2,1,0:T(8,128)} %get-tuple-element.128), channel_id=1, source_target_pairs={{1,0},{2,1},{3,2},{4,3},{5,4},{6,5},{7,6},{9,8},{10,9},{11,10},{12... | collective-permute-start | bytes 1572872 | tf_op jit(solution)/shard_map/while/body/eval_jaxpr/ppermute | solution.py:18
  218.4 6.7 %collective-permute-done.3 = f32[1,64,2048]{2,1,0:T(8,128)} collective-permute-done((f32[1,64,2048]{2,1,0:T(8,128)}, f32[1,64,2048]{2,1,0:T(8,128)}, u32[]{:S(2)}, u32[]{:S(2)}) %collective-permute-start.3) | collective-permute-done | bytes 524320 | tf_op jit(solution)/shard_map/while/body/eval_jaxpr/ppermute | solution.py:15
  225.1 3.4 collective-permute-done.4
  228.4 11.1 %fusion.40 = f32[4,64,2048]{2,1,0:T(8,128)} fusion(f32[4,64,2048]{2,1,0:T(8,128)} %get-tuple-element.148, f32[4,64,2048]{2,1,0:T(8,128)} %copy-done.2, f32[4,64,1]{2,1,0:T(8,128)S(1)} %get-tuple-element.125, f32[4,64,1]{2,1,0:T(8,128)S(1)} %get-tuple-element.126, f32[1,64,2048]{2,1,0:T(8,128)} %collective-permute-done.3, ...), kind=kLoop, calls=%fused_computation.14.clone.1 | loop fusion | flops 12058624 | bytes 12587009 | tf_op jit(solution)/shard_map/while/body/eval_jaxpr/add | solution.py:117
  241.4 1.9 collective-permute-start
  243.4 12.3 %collective-permute-done = bf16[4,64,2048]{2,1,0:T(8,128)(2,1)S(1)} collective-permute-done((bf16[4,64,2048]{2,1,0:T(8,128)(2,1)S(1)}, bf16[4,64,2048]{2,1,0:T(8,128)(2,1)S(1)}, u32[]{:S(2)}, u32[]{:S(2)}) %collective-permute-start) | collective-permute-done | bytes 1048608 | tf_op jit(solution)/shard_map/while/body/eval_jaxpr/ppermute | solution.py:26
  256.3 1.9 collective-permute-start.1
  258.2 4.8 %collective-permute-start.2 = (f32[1,64,2048]{2,1,0:T(8,128)S(1)}, f32[1,64,2048]{2,1,0:T(8,128)S(1)}, u32[]{:S(2)}, u32[]{:S(2)}) collective-permute-start(f32[1,64,2048]{2,1,0:T(8,128)S(1)} %get-tuple-element.124), channel_id=1, source_target_pairs={{1,0},{2,1},{3,2},{4,3},{5,4},{6,5},{7,6},{9,8},{10,9},{11,10},{12... | collective-permute-start | bytes 1572872 | tf_op jit(solution)/shard_map/while/body/eval_jaxpr/ppermute | solution.py:18
  263.1 8.4 %collective-permute-done.1 = f32[1,64,2048]{2,1,0:T(8,128)S(1)} collective-permute-done((f32[1,64,2048]{2,1,0:T(8,128)S(1)}, f32[1,64,2048]{2,1,0:T(8,128)S(1)}, u32[]{:S(2)}, u32[]{:S(2)}) %collective-permute-start.1) | collective-permute-done | bytes 524320 | tf_op jit(solution)/shard_map/while/body/eval_jaxpr/ppermute | solution.py:15
  271.5 3.1 collective-permute-done.2
  277.9 1.9 collective-permute-start.3
  279.8 4.8 %collective-permute-start.4 = (f32[1,64,2048]{2,1,0:T(8,128)}, f32[1,64,2048]{2,1,0:T(8,128)}, u32[]{:S(2)}, u32[]{:S(2)}) collective-permute-start(f32[1,64,2048]{2,1,0:T(8,128)} %get-tuple-element.128), channel_id=1, source_target_pairs={{1,0},{2,1},{3,2},{4,3},{5,4},{6,5},{7,6},{9,8},{10,9},{11,10},{12... | collective-permute-start | bytes 1572872 | tf_op jit(solution)/shard_map/while/body/eval_jaxpr/ppermute | solution.py:18
  285.7 12.4 %collective-permute-done.3 = f32[1,64,2048]{2,1,0:T(8,128)} collective-permute-done((f32[1,64,2048]{2,1,0:T(8,128)}, f32[1,64,2048]{2,1,0:T(8,128)}, u32[]{:S(2)}, u32[]{:S(2)}) %collective-permute-start.3) | collective-permute-done | bytes 524320 | tf_op jit(solution)/shard_map/while/body/eval_jaxpr/ppermute | solution.py:15
  298.1 3.1 collective-permute-done.4
  301.2 11.1 %fusion.40 = f32[4,64,2048]{2,1,0:T(8,128)} fusion(f32[4,64,2048]{2,1,0:T(8,128)} %get-tuple-element.148, f32[4,64,2048]{2,1,0:T(8,128)} %copy-done.2, f32[4,64,1]{2,1,0:T(8,128)S(1)} %get-tuple-element.125, f32[4,64,1]{2,1,0:T(8,128)S(1)} %get-tuple-element.126, f32[1,64,2048]{2,1,0:T(8,128)} %collective-permute-done.3, ...), kind=kLoop, calls=%fused_computation.14.clone.1 | loop fusion | flops 12058624 | bytes 12587009 | tf_op jit(solution)/shard_map/while/body/eval_jaxpr/add | solution.py:117
  312.3 1.9 convert_element_type.38
  314.2 5.9 %collective-permute-start = (bf16[4,64,2048]{2,1,0:T(8,128)(2,1)S(1)}, bf16[4,64,2048]{2,1,0:T(8,128)(2,1)S(1)}, u32[]{:S(2)}, u32[]{:S(2)}) collective-permute-start(bf16[4,64,2048]{2,1,0:T(8,128)(2,1)S(1)} %convert_element_type.38), channel_id=1, source_target_pairs={{8,0},{16,8},{24,16},{9,1},{17,9},{25,17},{10,2},{18,10},{26,18},{... | collective-permute-start | bytes 3145736 | tf_op jit(solution)/shard_map/while/body/eval_jaxpr/ppermute | solution.py:26
  320.1 12.3 %collective-permute-done = bf16[4,64,2048]{2,1,0:T(8,128)(2,1)S(1)} collective-permute-done((bf16[4,64,2048]{2,1,0:T(8,128)(2,1)S(1)}, bf16[4,64,2048]{2,1,0:T(8,128)(2,1)S(1)}, u32[]{:S(2)}, u32[]{:S(2)}) %collective-permute-start) | collective-permute-done | bytes 1048608 | tf_op jit(solution)/shard_map/while/body/eval_jaxpr/ppermute | solution.py:26
  333.0 1.9 collective-permute-start.1
  334.9 4.8 %collective-permute-start.2 = (f32[1,64,2048]{2,1,0:T(8,128)S(1)}, f32[1,64,2048]{2,1,0:T(8,128)S(1)}, u32[]{:S(2)}, u32[]{:S(2)}) collective-permute-start(f32[1,64,2048]{2,1,0:T(8,128)S(1)} %get-tuple-element.124), channel_id=1, source_target_pairs={{1,0},{2,1},{3,2},{4,3},{5,4},{6,5},{7,6},{9,8},{10,9},{11,10},{12... | collective-permute-start | bytes 1572872 | tf_op jit(solution)/shard_map/while/body/eval_jaxpr/ppermute | solution.py:18
  339.9 15.3 %collective-permute-done.1 = f32[1,64,2048]{2,1,0:T(8,128)S(1)} collective-permute-done((f32[1,64,2048]{2,1,0:T(8,128)S(1)}, f32[1,64,2048]{2,1,0:T(8,128)S(1)}, u32[]{:S(2)}, u32[]{:S(2)}) %collective-permute-start.1) | collective-permute-done | bytes 524320 | tf_op jit(solution)/shard_map/while/body/eval_jaxpr/ppermute | solution.py:15
  355.1 6.6 %collective-permute-done.2 = f32[1,64,2048]{2,1,0:T(8,128)S(1)} collective-permute-done((f32[1,64,2048]{2,1,0:T(8,128)S(1)}, f32[1,64,2048]{2,1,0:T(8,128)S(1)}, u32[]{:S(2)}, u32[]{:S(2)}) %collective-permute-start.2) | collective-permute-done | bytes 524320 | tf_op jit(solution)/shard_map/while/body/eval_jaxpr/ppermute | solution.py:18
  365.1 1.9 collective-permute-start.3
  367.0 4.8 %collective-permute-start.4 = (f32[1,64,2048]{2,1,0:T(8,128)}, f32[1,64,2048]{2,1,0:T(8,128)}, u32[]{:S(2)}, u32[]{:S(2)}) collective-permute-start(f32[1,64,2048]{2,1,0:T(8,128)} %get-tuple-element.128), channel_id=1, source_target_pairs={{1,0},{2,1},{3,2},{4,3},{5,4},{6,5},{7,6},{9,8},{10,9},{11,10},{12... | collective-permute-start | bytes 1572872 | tf_op jit(solution)/shard_map/while/body/eval_jaxpr/ppermute | solution.py:18
  372.9 6.7 %collective-permute-done.3 = f32[1,64,2048]{2,1,0:T(8,128)} collective-permute-done((f32[1,64,2048]{2,1,0:T(8,128)}, f32[1,64,2048]{2,1,0:T(8,128)}, u32[]{:S(2)}, u32[]{:S(2)}) %collective-permute-start.3) | collective-permute-done | bytes 524320 | tf_op jit(solution)/shard_map/while/body/eval_jaxpr/ppermute | solution.py:15
  379.6 3.4 collective-permute-done.4
  383.0 11.1 %fusion.40 = f32[4,64,2048]{2,1,0:T(8,128)} fusion(f32[4,64,2048]{2,1,0:T(8,128)} %get-tuple-element.148, f32[4,64,2048]{2,1,0:T(8,128)} %copy-done.2, f32[4,64,1]{2,1,0:T(8,128)S(1)} %get-tuple-element.125, f32[4,64,1]{2,1,0:T(8,128)S(1)} %get-tuple-element.126, f32[1,64,2048]{2,1,0:T(8,128)} %collective-permute-done.3, ...), kind=kLoop, calls=%fused_computation.14.clone.1 | loop fusion | flops 12058624 | bytes 12587009 | tf_op jit(solution)/shard_map/while/body/eval_jaxpr/add | solution.py:117
  (111 shorter events, 34.2 us)
Async XLA Ops:
  0.0 44.9 %copy-start = (bf16[96,128,128]{2,1,0:T(8,128)(2,1)S(1)}, bf16[96,128,128]{2,1,0:T(8,128)(2,1)}, u32[]{:S(2)}) copy-start(bf16[96,128,128]{2,1,0:T(8,128)(2,1)} %param.14) | copy-start | bytes 9437188
  4.3 23.9 %all-to-all-start = ((s32[32,1,6]{2,1,0:T(1,128)}), s32[32,1,6]{2,1,0:T(1,128)S(1)}, u32[]{:S(2)}, u32[]{:S(2)}) async-start(s32[32,1,6]{2,1,0:T(1,128)} %bitcast.3), calls=%async_computation | async-start | bytes 32768 | tf_op jit(solution)/shard_map/all_to_all | solution.py:92
  32.5 17.4 %copy-start.8 = (f32[96,128]{1,0:T(8,128)S(1)}, f32[96,128]{1,0:T(8,128)}, u32[]{:S(2)}) copy-start(f32[96,128]{1,0:T(8,128)} %param.15) | copy-start | bytes 147460
  32.5 17.4 %copy-start.9 = (f32[96,128]{1,0:T(8,128)S(1)}, f32[96,128]{1,0:T(8,128)}, u32[]{:S(2)}) copy-start(f32[96,128]{1,0:T(8,128)} %param.16) | copy-start | bytes 147460
  32.5 17.4 %copy-start.10 = (s32[96,128]{1,0:T(8,128)S(1)}, s32[96,128]{1,0:T(8,128)}, u32[]{:S(2)}) copy-start(s32[96,128]{1,0:T(8,128)} %param.17) | copy-start | bytes 147460
  32.5 11.8 %all-to-all-start.1 = ((f32[32,6,128]{2,1,0:T(8,128)}), f32[32,6,128]{2,1,0:T(8,128)S(1)}, u32[]{:S(2)}, u32[]{:S(2)}) async-start(f32[32,6,128]{2,1,0:T(8,128)} %reshape.60), calls=%async_computation.1 | async-start | bytes 262144 | tf_op jit(solution)/shard_map/all_to_all | solution.py:96
  54.0 10.4 %all-to-all-start.2 = ((f32[32,6,128]{2,1,0:T(8,128)}), f32[32,6,128]{2,1,0:T(8,128)S(1)}, u32[]{:S(2)}, u32[]{:S(2)}) async-start(f32[32,6,128]{2,1,0:T(8,128)} %reshape.62), calls=%async_computation.2 | async-start | bytes 262144 | tf_op jit(solution)/shard_map/all_to_all | solution.py:101
  87.4 16.7 %copy-start.3 = (bf16[4,64,2048]{2,1,0:T(8,128)(2,1)S(1)}, bf16[4,64,2048]{2,1,0:T(8,128)(2,1)}, u32[]{:S(2)}) copy-start(bf16[4,64,2048]{2,1,0:T(8,128)(2,1)} %get-tuple-element.146) | copy-start | bytes 3145732 | tf_op jit(solution)/shard_map/while
  87.4 16.7 %copy-start.5 = (f32[4,64,2048]{2,1,0:T(8,128)S(1)}, f32[4,64,2048]{2,1,0:T(8,128)}, u32[]{:S(2)}) copy-start(f32[4,64,2048]{2,1,0:T(8,128)} %get-tuple-element.147) | copy-start | bytes 6291460 | tf_op jit(solution)/shard_map/while
  89.2 14.8 %collective-permute-start = (bf16[4,64,2048]{2,1,0:T(8,128)(2,1)S(1)}, bf16[4,64,2048]{2,1,0:T(8,128)(2,1)S(1)}, u32[]{:S(2)}, u32[]{:S(2)}) collective-permute-start(bf16[4,64,2048]{2,1,0:T(8,128)(2,1)S(1)} %convert_element_type.38), channel_id=1, source_target_pairs={{8,0},{16,8},{24,16},{9,1},{17,9},{25,17},{10,2},{18,10},{26,18},{... | collective-permute-start | bytes 3145736 | tf_op jit(solution)/shard_map/while/body/eval_jaxpr/ppermute | solution.py:26
  104.1 18.3 %copy-start.4 = (bf16[4,64,2048]{2,1,0:T(8,128)(2,1)}, bf16[4,64,2048]{2,1,0:T(8,128)(2,1)S(1)}, u32[]{:S(2)}) copy-start(bf16[4,64,2048]{2,1,0:T(8,128)(2,1)S(1)} %collective-permute-done) | copy-start | bytes 3145732 | tf_op jit(solution)/shard_map/while
  104.6 19.4 %copy-start.1 = (f32[4,64,2048]{2,1,0:T(8,128)}, f32[4,64,2048]{2,1,0:T(8,128)S(1)}, u32[]{:S(2)}) copy-start(f32[4,64,2048]{2,1,0:T(8,128)S(1)} %convert_multiply_fusion.2) | copy-start | bytes 6291460 | tf_op jit(solution)/shard_map/while
  104.7 15.8 %collective-permute-start.1 = (f32[1,64,2048]{2,1,0:T(8,128)S(1)}, f32[1,64,2048]{2,1,0:T(8,128)S(1)}, u32[]{:S(2)}, u32[]{:S(2)}) collective-permute-start(f32[1,64,2048]{2,1,0:T(8,128)S(1)} %get-tuple-element.123), channel_id=1, source_target_pairs={{0,1},{1,2},{2,3},{3,4},{4,5},{5,6},{6,7},{8,9},{9,10},{10,11},{11... | collective-permute-start | bytes 1572872 | tf_op jit(solution)/shard_map/while/body/eval_jaxpr/ppermute | solution.py:15
  108.2 14.2 %collective-permute-start.2 = (f32[1,64,2048]{2,1,0:T(8,128)S(1)}, f32[1,64,2048]{2,1,0:T(8,128)S(1)}, u32[]{:S(2)}, u32[]{:S(2)}) collective-permute-start(f32[1,64,2048]{2,1,0:T(8,128)S(1)} %get-tuple-element.124), channel_id=1, source_target_pairs={{1,0},{2,1},{3,2},{4,3},{5,4},{6,5},{7,6},{9,8},{10,9},{11,10},{12... | collective-permute-start | bytes 1572872 | tf_op jit(solution)/shard_map/while/body/eval_jaxpr/ppermute | solution.py:18
  120.5 3.5 copy-start.6
  122.4 1.6 copy-start.7
  124.0 1.7 copy-start.2
  125.7 13.0 %collective-permute-start.3 = (f32[1,64,2048]{2,1,0:T(8,128)}, f32[1,64,2048]{2,1,0:T(8,128)}, u32[]{:S(2)}, u32[]{:S(2)}) collective-permute-start(f32[1,64,2048]{2,1,0:T(8,128)} %get-tuple-element.127), channel_id=1, source_target_pairs={{0,1},{1,2},{2,3},{3,4},{4,5},{5,6},{6,7},{8,9},{9,10},{10,11},{11... | collective-permute-start | bytes 1572872 | tf_op jit(solution)/shard_map/while/body/eval_jaxpr/ppermute | solution.py:15
  128.2 20.2 %collective-permute-start.4 = (f32[1,64,2048]{2,1,0:T(8,128)}, f32[1,64,2048]{2,1,0:T(8,128)}, u32[]{:S(2)}, u32[]{:S(2)}) collective-permute-start(f32[1,64,2048]{2,1,0:T(8,128)} %get-tuple-element.128), channel_id=1, source_target_pairs={{1,0},{2,1},{3,2},{4,3},{5,4},{6,5},{7,6},{9,8},{10,9},{11,10},{12... | collective-permute-start | bytes 1572872 | tf_op jit(solution)/shard_map/while/body/eval_jaxpr/ppermute | solution.py:18
  159.5 19.2 %copy-start.3 = (bf16[4,64,2048]{2,1,0:T(8,128)(2,1)S(1)}, bf16[4,64,2048]{2,1,0:T(8,128)(2,1)}, u32[]{:S(2)}) copy-start(bf16[4,64,2048]{2,1,0:T(8,128)(2,1)} %get-tuple-element.146) | copy-start | bytes 3145732 | tf_op jit(solution)/shard_map/while
  159.5 19.2 %copy-start.5 = (f32[4,64,2048]{2,1,0:T(8,128)S(1)}, f32[4,64,2048]{2,1,0:T(8,128)}, u32[]{:S(2)}) copy-start(f32[4,64,2048]{2,1,0:T(8,128)} %get-tuple-element.147) | copy-start | bytes 6291460 | tf_op jit(solution)/shard_map/while
  161.4 17.3 %collective-permute-start = (bf16[4,64,2048]{2,1,0:T(8,128)(2,1)S(1)}, bf16[4,64,2048]{2,1,0:T(8,128)(2,1)S(1)}, u32[]{:S(2)}, u32[]{:S(2)}) collective-permute-start(bf16[4,64,2048]{2,1,0:T(8,128)(2,1)S(1)} %convert_element_type.38), channel_id=1, source_target_pairs={{8,0},{16,8},{24,16},{9,1},{17,9},{25,17},{10,2},{18,10},{26,18},{... | collective-permute-start | bytes 3145736 | tf_op jit(solution)/shard_map/while/body/eval_jaxpr/ppermute | solution.py:26
  178.7 28.6 %copy-start.4 = (bf16[4,64,2048]{2,1,0:T(8,128)(2,1)}, bf16[4,64,2048]{2,1,0:T(8,128)(2,1)S(1)}, u32[]{:S(2)}) copy-start(bf16[4,64,2048]{2,1,0:T(8,128)(2,1)S(1)} %collective-permute-done) | copy-start | bytes 3145732 | tf_op jit(solution)/shard_map/while
  179.2 29.7 %copy-start.1 = (f32[4,64,2048]{2,1,0:T(8,128)}, f32[4,64,2048]{2,1,0:T(8,128)S(1)}, u32[]{:S(2)}) copy-start(f32[4,64,2048]{2,1,0:T(8,128)S(1)} %convert_multiply_fusion.2) | copy-start | bytes 6291460 | tf_op jit(solution)/shard_map/while
  179.3 12.1 %collective-permute-start.1 = (f32[1,64,2048]{2,1,0:T(8,128)S(1)}, f32[1,64,2048]{2,1,0:T(8,128)S(1)}, u32[]{:S(2)}, u32[]{:S(2)}) collective-permute-start(f32[1,64,2048]{2,1,0:T(8,128)S(1)} %get-tuple-element.123), channel_id=1, source_target_pairs={{0,1},{1,2},{2,3},{3,4},{4,5},{5,6},{6,7},{8,9},{9,10},{10,11},{11... | collective-permute-start | bytes 1572872 | tf_op jit(solution)/shard_map/while/body/eval_jaxpr/ppermute | solution.py:15
  181.2 26.0 %collective-permute-start.2 = (f32[1,64,2048]{2,1,0:T(8,128)S(1)}, f32[1,64,2048]{2,1,0:T(8,128)S(1)}, u32[]{:S(2)}, u32[]{:S(2)}) collective-permute-start(f32[1,64,2048]{2,1,0:T(8,128)S(1)} %get-tuple-element.124), channel_id=1, source_target_pairs={{1,0},{2,1},{3,2},{4,3},{5,4},{6,5},{7,6},{9,8},{10,9},{11,10},{12... | collective-permute-start | bytes 1572872 | tf_op jit(solution)/shard_map/while/body/eval_jaxpr/ppermute | solution.py:18
  191.4 17.5 %copy-start.6 = (f32[1,64,2048]{2,1,0:T(8,128)}, f32[1,64,2048]{2,1,0:T(8,128)S(1)}, u32[]{:S(2)}) copy-start(f32[1,64,2048]{2,1,0:T(8,128)S(1)} %collective-permute-done.1) | copy-start | bytes 1572868 | tf_op jit(solution)/shard_map/while
  207.2 1.6 copy-start.7
  208.9 1.7 copy-start.2
  210.5 14.5 %collective-permute-start.3 = (f32[1,64,2048]{2,1,0:T(8,128)}, f32[1,64,2048]{2,1,0:T(8,128)}, u32[]{:S(2)}, u32[]{:S(2)}) collective-permute-start(f32[1,64,2048]{2,1,0:T(8,128)} %get-tuple-element.127), channel_id=1, source_target_pairs={{0,1},{1,2},{2,3},{3,4},{4,5},{5,6},{6,7},{8,9},{9,10},{10,11},{11... | collective-permute-start | bytes 1572872 | tf_op jit(solution)/shard_map/while/body/eval_jaxpr/ppermute | solution.py:15
  212.5 16.0 %collective-permute-start.4 = (f32[1,64,2048]{2,1,0:T(8,128)}, f32[1,64,2048]{2,1,0:T(8,128)}, u32[]{:S(2)}, u32[]{:S(2)}) collective-permute-start(f32[1,64,2048]{2,1,0:T(8,128)} %get-tuple-element.128), channel_id=1, source_target_pairs={{1,0},{2,1},{3,2},{4,3},{5,4},{6,5},{7,6},{9,8},{10,9},{11,10},{12... | collective-permute-start | bytes 1572872 | tf_op jit(solution)/shard_map/while/body/eval_jaxpr/ppermute | solution.py:18
  239.5 16.1 %copy-start.3 = (bf16[4,64,2048]{2,1,0:T(8,128)(2,1)S(1)}, bf16[4,64,2048]{2,1,0:T(8,128)(2,1)}, u32[]{:S(2)}) copy-start(bf16[4,64,2048]{2,1,0:T(8,128)(2,1)} %get-tuple-element.146) | copy-start | bytes 3145732 | tf_op jit(solution)/shard_map/while
  239.5 16.1 %copy-start.5 = (f32[4,64,2048]{2,1,0:T(8,128)S(1)}, f32[4,64,2048]{2,1,0:T(8,128)}, u32[]{:S(2)}) copy-start(f32[4,64,2048]{2,1,0:T(8,128)} %get-tuple-element.147) | copy-start | bytes 6291460 | tf_op jit(solution)/shard_map/while
  241.4 14.2 %collective-permute-start = (bf16[4,64,2048]{2,1,0:T(8,128)(2,1)S(1)}, bf16[4,64,2048]{2,1,0:T(8,128)(2,1)S(1)}, u32[]{:S(2)}, u32[]{:S(2)}) collective-permute-start(bf16[4,64,2048]{2,1,0:T(8,128)(2,1)S(1)} %convert_element_type.38), channel_id=1, source_target_pairs={{8,0},{16,8},{24,16},{9,1},{17,9},{25,17},{10,2},{18,10},{26,18},{... | collective-permute-start | bytes 3145736 | tf_op jit(solution)/shard_map/while/body/eval_jaxpr/ppermute | solution.py:26
  255.7 18.9 %copy-start.4 = (bf16[4,64,2048]{2,1,0:T(8,128)(2,1)}, bf16[4,64,2048]{2,1,0:T(8,128)(2,1)S(1)}, u32[]{:S(2)}) copy-start(bf16[4,64,2048]{2,1,0:T(8,128)(2,1)S(1)} %collective-permute-done) | copy-start | bytes 3145732 | tf_op jit(solution)/shard_map/while
  256.2 20.0 %copy-start.1 = (f32[4,64,2048]{2,1,0:T(8,128)}, f32[4,64,2048]{2,1,0:T(8,128)S(1)}, u32[]{:S(2)}) copy-start(f32[4,64,2048]{2,1,0:T(8,128)S(1)} %convert_multiply_fusion.2) | copy-start | bytes 6291460 | tf_op jit(solution)/shard_map/while
  256.3 15.2 %collective-permute-start.1 = (f32[1,64,2048]{2,1,0:T(8,128)S(1)}, f32[1,64,2048]{2,1,0:T(8,128)S(1)}, u32[]{:S(2)}, u32[]{:S(2)}) collective-permute-start(f32[1,64,2048]{2,1,0:T(8,128)S(1)} %get-tuple-element.123), channel_id=1, source_target_pairs={{0,1},{1,2},{2,3},{3,4},{4,5},{5,6},{6,7},{8,9},{9,10},{10,11},{11... | collective-permute-start | bytes 1572872 | tf_op jit(solution)/shard_map/while/body/eval_jaxpr/ppermute | solution.py:15
  258.2 16.4 %collective-permute-start.2 = (f32[1,64,2048]{2,1,0:T(8,128)S(1)}, f32[1,64,2048]{2,1,0:T(8,128)S(1)}, u32[]{:S(2)}, u32[]{:S(2)}) collective-permute-start(f32[1,64,2048]{2,1,0:T(8,128)S(1)} %get-tuple-element.124), channel_id=1, source_target_pairs={{1,0},{2,1},{3,2},{4,3},{5,4},{6,5},{7,6},{9,8},{10,9},{11,10},{12... | collective-permute-start | bytes 1572872 | tf_op jit(solution)/shard_map/while/body/eval_jaxpr/ppermute | solution.py:18
  271.5 4.7 %copy-start.6 = (f32[1,64,2048]{2,1,0:T(8,128)}, f32[1,64,2048]{2,1,0:T(8,128)S(1)}, u32[]{:S(2)}) copy-start(f32[1,64,2048]{2,1,0:T(8,128)S(1)} %collective-permute-done.1) | copy-start | bytes 1572868 | tf_op jit(solution)/shard_map/while
  274.6 1.6 copy-start.7
  276.3 1.7 copy-start.2
  277.9 20.2 %collective-permute-start.3 = (f32[1,64,2048]{2,1,0:T(8,128)}, f32[1,64,2048]{2,1,0:T(8,128)}, u32[]{:S(2)}, u32[]{:S(2)}) collective-permute-start(f32[1,64,2048]{2,1,0:T(8,128)} %get-tuple-element.127), channel_id=1, source_target_pairs={{0,1},{1,2},{2,3},{3,4},{4,5},{5,6},{6,7},{8,9},{9,10},{10,11},{11... | collective-permute-start | bytes 1572872 | tf_op jit(solution)/shard_map/while/body/eval_jaxpr/ppermute | solution.py:15
  279.8 21.4 %collective-permute-start.4 = (f32[1,64,2048]{2,1,0:T(8,128)}, f32[1,64,2048]{2,1,0:T(8,128)}, u32[]{:S(2)}, u32[]{:S(2)}) collective-permute-start(f32[1,64,2048]{2,1,0:T(8,128)} %get-tuple-element.128), channel_id=1, source_target_pairs={{1,0},{2,1},{3,2},{4,3},{5,4},{6,5},{7,6},{9,8},{10,9},{11,10},{12... | collective-permute-start | bytes 1572872 | tf_op jit(solution)/shard_map/while/body/eval_jaxpr/ppermute | solution.py:18
  312.3 20.1 %copy-start.3 = (bf16[4,64,2048]{2,1,0:T(8,128)(2,1)S(1)}, bf16[4,64,2048]{2,1,0:T(8,128)(2,1)}, u32[]{:S(2)}) copy-start(bf16[4,64,2048]{2,1,0:T(8,128)(2,1)} %get-tuple-element.146) | copy-start | bytes 3145732 | tf_op jit(solution)/shard_map/while
  312.3 20.1 %copy-start.5 = (f32[4,64,2048]{2,1,0:T(8,128)S(1)}, f32[4,64,2048]{2,1,0:T(8,128)}, u32[]{:S(2)}) copy-start(f32[4,64,2048]{2,1,0:T(8,128)} %get-tuple-element.147) | copy-start | bytes 6291460 | tf_op jit(solution)/shard_map/while
  314.2 18.2 %collective-permute-start = (bf16[4,64,2048]{2,1,0:T(8,128)(2,1)S(1)}, bf16[4,64,2048]{2,1,0:T(8,128)(2,1)S(1)}, u32[]{:S(2)}, u32[]{:S(2)}) collective-permute-start(bf16[4,64,2048]{2,1,0:T(8,128)(2,1)S(1)} %convert_element_type.38), channel_id=1, source_target_pairs={{8,0},{16,8},{24,16},{9,1},{17,9},{25,17},{10,2},{18,10},{26,18},{... | collective-permute-start | bytes 3145736 | tf_op jit(solution)/shard_map/while/body/eval_jaxpr/ppermute | solution.py:26
  332.4 29.4 %copy-start.4 = (bf16[4,64,2048]{2,1,0:T(8,128)(2,1)}, bf16[4,64,2048]{2,1,0:T(8,128)(2,1)S(1)}, u32[]{:S(2)}) copy-start(bf16[4,64,2048]{2,1,0:T(8,128)(2,1)S(1)} %collective-permute-done) | copy-start | bytes 3145732 | tf_op jit(solution)/shard_map/while
  332.9 30.4 %copy-start.1 = (f32[4,64,2048]{2,1,0:T(8,128)}, f32[4,64,2048]{2,1,0:T(8,128)S(1)}, u32[]{:S(2)}) copy-start(f32[4,64,2048]{2,1,0:T(8,128)S(1)} %convert_multiply_fusion.2) | copy-start | bytes 6291460 | tf_op jit(solution)/shard_map/while
  333.0 22.1 %collective-permute-start.1 = (f32[1,64,2048]{2,1,0:T(8,128)S(1)}, f32[1,64,2048]{2,1,0:T(8,128)S(1)}, u32[]{:S(2)}, u32[]{:S(2)}) collective-permute-start(f32[1,64,2048]{2,1,0:T(8,128)S(1)} %get-tuple-element.123), channel_id=1, source_target_pairs={{0,1},{1,2},{2,3},{3,4},{4,5},{5,6},{6,7},{8,9},{9,10},{10,11},{11... | collective-permute-start | bytes 1572872 | tf_op jit(solution)/shard_map/while/body/eval_jaxpr/ppermute | solution.py:15
  334.9 26.8 %collective-permute-start.2 = (f32[1,64,2048]{2,1,0:T(8,128)S(1)}, f32[1,64,2048]{2,1,0:T(8,128)S(1)}, u32[]{:S(2)}, u32[]{:S(2)}) collective-permute-start(f32[1,64,2048]{2,1,0:T(8,128)S(1)} %get-tuple-element.124), channel_id=1, source_target_pairs={{1,0},{2,1},{3,2},{4,3},{5,4},{6,5},{7,6},{9,8},{10,9},{11,10},{12... | collective-permute-start | bytes 1572872 | tf_op jit(solution)/shard_map/while/body/eval_jaxpr/ppermute | solution.py:18
  355.1 8.2 %copy-start.6 = (f32[1,64,2048]{2,1,0:T(8,128)}, f32[1,64,2048]{2,1,0:T(8,128)S(1)}, u32[]{:S(2)}) copy-start(f32[1,64,2048]{2,1,0:T(8,128)S(1)} %collective-permute-done.1) | copy-start | bytes 1572868 | tf_op jit(solution)/shard_map/while
  361.7 1.6 copy-start.7
  363.4 1.7 copy-start.2
  365.1 14.5 %collective-permute-start.3 = (f32[1,64,2048]{2,1,0:T(8,128)}, f32[1,64,2048]{2,1,0:T(8,128)}, u32[]{:S(2)}, u32[]{:S(2)}) collective-permute-start(f32[1,64,2048]{2,1,0:T(8,128)} %get-tuple-element.127), channel_id=1, source_target_pairs={{0,1},{1,2},{2,3},{3,4},{4,5},{5,6},{6,7},{8,9},{9,10},{10,11},{11... | collective-permute-start | bytes 1572872 | tf_op jit(solution)/shard_map/while/body/eval_jaxpr/ppermute | solution.py:15
  367.0 16.0 %collective-permute-start.4 = (f32[1,64,2048]{2,1,0:T(8,128)}, f32[1,64,2048]{2,1,0:T(8,128)}, u32[]{:S(2)}, u32[]{:S(2)}) collective-permute-start(f32[1,64,2048]{2,1,0:T(8,128)} %get-tuple-element.128), channel_id=1, source_target_pairs={{1,0},{2,1},{3,2},{4,3},{5,4},{6,5},{7,6},{9,8},{10,9},{11,10},{12... | collective-permute-start | bytes 1572872 | tf_op jit(solution)/shard_map/while/body/eval_jaxpr/ppermute | solution.py:18
where the time goes:
time: 392 us; the launch traced here: 394 us
  waiting for transfers between devices  176 us (45%)
  starting transfers between devices  86 us (22%)
  other arithmetic  66.2 us (17%)
  local copies, waits for them, and re-layouts  57.3 us (15%)
  matrix products  7.49 us (2%)
    ppermute x8, waiting for transfers between devices, extended(): lax.ppermute(lax.slice_in_dim(block, block.shape[dim] - width, None, axis...  68.2 us
    ppermute x4, waiting for transfers between devices, passed_along(): return lax.ppermute(block, axis, route)  49.2 us
    ppermute x8, waiting for transfers between devices, extended(): lax.ppermute(lax.slice_in_dim(block, 0, width, axis=dim), axis, backward)  46.9 us
    add x4, other arithmetic, advance(): return forcing + propagate(incoming, coeff_own)  44.3 us
    ppermute x8, starting transfers between devices, extended(): lax.ppermute(lax.slice_in_dim(block, 0, width, axis=dim), axis, backward)  37 us
    ppermute x8, starting transfers between devices, extended(): lax.ppermute(lax.slice_in_dim(block, block.shape[dim] - width, None, axis...  17.5 us
    ppermute x4, starting transfers between devices, passed_along(): return lax.ppermute(block, axis, route)  15.3 us
    unnamed x11, local copies, waits for them, and re-layouts  11.5 us
  transfers between devices with their start and end apart: 23, of which 22 were waited for; matrix products, arithmetic and copies ran while one was open for 6% of the time, Pallas kernels for 0%

commit v1 on v0

v1 whole, which is shorter than its diff:
```python
import jax
import jax.numpy as jnp
from jax import lax
from jax.experimental import pallas as pl
from jax.experimental.pallas import tpu as pltpu
from jax.sharding import PartitionSpec as P

TW = 2
SUB = 2
LANES = 128
F32 = jnp.float32
BF16 = jnp.bfloat16
COEFF = jnp.float16

SMEM = pl.BlockSpec(memory_space=pltpu.SMEM)
VMEM = pl.BlockSpec(memory_space=pltpu.VMEM)


def route(owner, tile, sections, bands, slots):
    devices = sections * bands
    blocks = owner.shape[0]
    per_target = sections * slots

    def body(owner_ref, tile_ref, slot_ref, table_ref, used_ref):
        def clear(i, c):
            for j in range(per_target):
                table_ref[i * per_target + j] = -1
            used_ref[i] = 0
            return c

        lax.fori_loop(0, devices, clear, 0)

        def put(k, c):
            target = owner_ref[k]
            rank = used_ref[target]
            used_ref[target] = rank + 1
            slot_ref[k] = target * slots + rank
            section = target // bands
            band = target % bands
            for other in range(sections):
                at = ((other * bands + band) * sections + section) * slots + rank
                table_ref[at] = tile_ref[k]
            return c

        lax.fori_loop(0, blocks, put, 0)

    return pl.pallas_call(
        body,
        name="route",
        in_specs=[SMEM, SMEM],
        out_specs=[SMEM, SMEM],
        out_shape=[
            jax.ShapeDtypeStruct((blocks,), jnp.int32),
            jax.ShapeDtypeStruct((devices * per_target,), jnp.int32),
        ],
        scratch_shapes=[pltpu.SMEM((devices,), jnp.int32)],
    )(owner, tile)


def fetch_states(place, ids, traj, sections, slots):
    rows, levels, nlon = traj.shape
    per_row = nlon // TW
    pairs = LANES // TW
    per_target = sections * slots
    count = ids.shape[0] // sections

    def body(place_ref, ids_ref, traj_ref, out_ref, pairs_ref):
        lane = lax.broadcasted_iota(jnp.int32, (levels, LANES), 1)
        which = lax.broadcasted_iota(jnp.int32, (levels, LANES), 0)
        pick = (lane // TW == which).astype(BF16)
        mine = place_ref[0] * slots

        for group in range(count // pairs):

            def one(k, gathered):
                i = group * pairs + k
                at = (i // slots) * per_target + mine + i % slots
                tile = jnp.maximum(ids_ref[at], 0)
                row = tile // per_row
                column = tile % per_row
                start = pl.multiple_of(column // pairs * LANES, LANES)
                shift = (TW * k + LANES - column % pairs * TW) % LANES
                turned = pltpu.roll(traj_ref[row, :, pl.ds(start, LANES)], shift, 1)
                return jnp.where(lane // TW == k, turned, gathered)

            gathered = lax.fori_loop(
                0, pairs, one, jnp.zeros((levels, LANES), F32), unroll=8
            )
            pairs_ref[...] = sum(
                lax.dot_general(
                    piece.astype(BF16), pick, (((0,), (0,)), ((), ())),
                    preferred_element_type=F32,
                )
                for piece in split3(gathered)
            )
            even = pairs_ref[pl.ds(0, pairs, stride=TW), :]
            odd = pairs_ref[pl.ds(1, pairs, stride=TW), :]
            out_ref[group * pairs : (group + 1) * pairs, :] = jnp.where(
                lane[:pairs] % TW == 0, even, odd
            )

    return pl.pallas_call(
        body,
        name="fetch_states",
        in_specs=[SMEM, SMEM, VMEM],
        out_specs=VMEM,
        out_shape=jax.ShapeDtypeStruct((count, LANES), F32),
        scratch_shapes=[pltpu.VMEM((LANES, LANES), F32)],
    )(place, ids, traj)


def split3(x):
    a = x.astype(BF16).astype(F32)
    r = x - a
    b = r.astype(BF16).astype(F32)
    return a, b, r - b


def block_terms(slot, jac, found, value, weight, valid, sections, slots):
    blocks, channels, entries = jac.shape
    count = found.shape[0]
    part = LANES // sections
    group = 24 if blocks % 24 == 0 else blocks
    steps = blocks // group
    band_rows = count // sections

    def stacked(parts, k, which):
        picked = jnp.where(
            which == 0,
            jnp.broadcast_to(parts[0][k : k + 1], which.shape),
            jnp.where(
                which == 1,
                jnp.broadcast_to(parts[1][k : k + 1], which.shape),
                jnp.where(
                    which == 2, jnp.broadcast_to(parts[2][k : k + 1], which.shape), 0.0
                ),
            ),
        )
        return picked.astype(BF16)

    def body(slot_ref, jac_ref, found_ref, value_ref, weight_ref, valid_ref, out_ref, placed_ref, rows_ref):
        step = pl.program_id(0)
        which = lax.broadcasted_iota(jnp.int32, (16, LANES), 0)

        @pl.when(step == 0)
        def _():
            placed_ref[...] = jnp.zeros_like(placed_ref)

        base = step * group
        for k in range(group):
            rows_ref[k : k + 1, :] = found_ref[pl.ds(slot_ref[base + k], 1), :]
        state = split3(rows_ref[...])
        preds = []
        for k in range(group):
            got = lax.dot_general(
                stacked(state, k, which), jac_ref[k], (((1,), (1,)), ((), ())),
                preferred_element_type=F32,
            )
            preds.append(jnp.sum(got, axis=0, keepdims=True))
        pred = jnp.concatenate(preds, axis=0)
        gain = weight_ref[...] * valid_ref[...].astype(F32)
        resid = split3(gain * (value_ref[...] - pred))
        for k in range(group):
            got = lax.dot_general(
                stacked(resid, k, which), jac_ref[k], (((1,), (0,)), ((), ())),
                preferred_element_type=F32,
            )
            placed_ref[pl.ds(slot_ref[base + k], 1), :] = jnp.sum(got, axis=0, keepdims=True)

        @pl.when(step == steps - 1)
        def _():
            lane = lax.broadcasted_iota(jnp.int32, (band_rows, LANES), 1)
            for j in range(sections):
                total = jnp.zeros((band_rows, LANES), F32)
                for s in range(sections):
                    rows = placed_ref[s * band_rows : (s + 1) * band_rows, :]
                    shift = part * (s - j) % LANES
                    moved = pltpu.roll(rows, shift, 1) if shift else rows
                    total = jnp.where(lane // part == s, moved, total)
                out_ref[j * band_rows : (j + 1) * band_rows, :] = total

    rows_of = pl.BlockSpec((group, channels), lambda i: (i, 0))
    whole = pl.BlockSpec((count, LANES), lambda i: (0, 0))
    return pl.pallas_call(
        body,
        name="block_terms",
        grid=(steps,),
        in_specs=[
            SMEM,
            pl.BlockSpec((group, channels, entries), lambda i: (i, 0, 0)),
            whole,
            rows_of,
            rows_of,
            rows_of,
        ],
        out_specs=whole,
        out_shape=jax.ShapeDtypeStruct((count, LANES), F32),
        scratch_shapes=[pltpu.VMEM((count, LANES), F32), pltpu.VMEM((group, LANES), F32)],
    )(slot, jac, found, value, weight, valid)


def spread_forcing(ids, received, section, sections, slots, shape):
    rows, share, nlon = shape
    per_row = nlon // TW
    pairs = LANES // TW
    per_target = sections * slots
    count = received.shape[0]
    first = section * (LANES // sections)

    def body(ids_ref, recv_ref, out_ref, pairs_ref, terms_ref):
        out_ref[...] = jnp.zeros_like(out_ref)
        lane = lax.broadcasted_iota(jnp.int32, (share, LANES), 1)
        level = lax.broadcasted_iota(jnp.int32, (share, LANES), 0)
        pick = (lane // TW == level + first // TW).astype(BF16)
        parity = lax.broadcasted_iota(jnp.int32, (pairs, LANES), 1) % TW
        for group in range(count // pairs):
            block = recv_ref[group * pairs : (group + 1) * pairs, :]
            for j in range(TW):
                pairs_ref[pl.ds(j, pairs, stride=TW), :] = jnp.where(
                    parity == j, block, 0.0
                )
            terms_ref[group] = sum(
                lax.dot_general(
                    pick, piece.astype(BF16), (((1,), (1,)), ((), ())),
                    preferred_element_type=F32,
                )
                for piece in split3(pairs_ref[...])
            )

        def one(i, c):
            at = (i // slots) * per_target + section * slots + i % slots
            tile = jnp.maximum(ids_ref[at], 0)
            row = tile // per_row
            column = tile % per_row
            start = pl.multiple_of(column // pairs * LANES, LANES)
            off = column % pairs
            shift = (off + pairs - i % pairs) % pairs * TW
            turned = pltpu.roll(terms_ref[i // pairs], shift, 1)
            out_ref[row, :, pl.ds(start, LANES)] += jnp.where(
                lane // TW == off, turned, 0.0
            )
            return c

        lax.fori_loop(0, count, one, 0, unroll=8)

    return pl.pallas_call(
        body,
        name=f"spread_forcing_{section}",
        in_specs=[SMEM, VMEM],
        out_specs=VMEM,
        out_shape=jax.ShapeDtypeStruct(shape, F32),
        scratch_shapes=[
            pltpu.VMEM((LANES, LANES), F32),
            pltpu.VMEM((count // pairs, share, LANES), F32),
        ],
    )(ids, received)


def sweep(held, low, high, coeff, coeff_low, coeff_high, forcing, section):
    rows, share, nlon = held.shape
    halo = SUB

    def body(held_ref, low_ref, high_ref, c_ref, cl_ref, ch_ref, f_ref, out_ref):
        def of(own, lower, upper, r):
            if r < 0:
                return lower[r + halo].astype(F32)
            if r >= rows:
                return upper[r - rows].astype(F32)
            return own[r].astype(F32)

        field = {r: of(held_ref, low_ref, high_ref, r) for r in range(-halo, rows + halo)}
        for step in range(SUB):
            edge = halo - step
            weighted = {
                r: of(c_ref.at[0], cl_ref.at[0], ch_ref.at[0], r) * field[r]
                for r in range(-edge, rows + edge)
            }
            field = {
                r: field[r]
                + weighted[r + 1]
                + weighted[r - 1]
                + pltpu.roll(weighted[r], 1, 1)
                + pltpu.roll(weighted[r], nlon - 1, 1)
                - 4.0 * weighted[r]
                for r in range(-edge + 1, rows + edge - 1)
            }
        for r in range(rows):
            out_ref[r] = (f_ref[r] + field[r]).astype(out_ref.dtype)

    def full(shape):
        return pl.BlockSpec(shape, lambda i: (0,) * len(shape))

    def pick(shape):
        return pl.BlockSpec((1,) + shape[1:], lambda i: (section, 0, 0, 0))

    return pl.pallas_call(
        body,
        name=f"sweep_{section}",
        grid=(1,),
        in_specs=[
            full(held.shape), full(low.shape), full(high.shape),
            pick(coeff.shape), pick(coeff_low.shape), pick(coeff_high.shape),
            full(forcing.shape),
        ],
        out_specs=full(held.shape),
        out_shape=jax.ShapeDtypeStruct(held.shape, BF16),
    )(held, low, high, coeff, coeff_low, coeff_high, forcing)


def edges(block, dim, width):
    count = lax.axis_size("lat")
    forward = [(i, i + 1) for i in range(count - 1)]
    backward = [(j, i) for i, j in forward]
    size = block.shape[dim]
    low = lax.ppermute(lax.slice_in_dim(block, size - width, size, axis=dim), "lat", forward)
    high = lax.ppermute(lax.slice_in_dim(block, 0, width, axis=dim), "lat", backward)
    return low, high


def per_device(
    trajectory,
    diffusivity,
    adjoint_end,
    obs_jac,
    obs_value,
    obs_weight,
    obs_valid,
    obs_owner,
    obs_tile,
):
    traj = trajectory[0]
    rows, levels, nlon = traj.shape
    sections = lax.axis_size("tm")
    bands = lax.axis_size("lat")
    devices = sections * bands
    blocks = obs_owner.shape[0]
    slots = max(2, 2 * blocks // devices)
    share = levels // sections
    me = lax.axis_index("tm")
    every = ("tm", "lat")

    def exchange(x):
        return lax.all_to_all(x, every, split_axis=0, concat_axis=0, tiled=True)

    coeff = lax.all_to_all(
        diffusivity[0].astype(COEFF).reshape(rows, sections, share, nlon), "tm", 1, 0
    )
    coeff_low, coeff_high = edges(coeff, 1, SUB)
    coeff, coeff_low, coeff_high = (c.astype(F32) for c in (coeff, coeff_low, coeff_high))
    held = lax.dynamic_slice_in_dim(adjoint_end, me * share, share, axis=1)

    slot, table = route(obs_owner.reshape(blocks), obs_tile, sections, bands, slots)
    ids = exchange(table.reshape(devices, sections * slots)).reshape(-1)
    asked = fetch_states(me.astype(jnp.int32).reshape(1), ids, traj, sections, slots)
    found = exchange(asked.reshape(devices, slots, LANES)).reshape(devices * slots, LANES)
    terms = block_terms(
        slot, obs_jac, found, obs_value, obs_weight, obs_valid, sections, slots
    )
    received = exchange(terms.reshape(devices, slots, LANES)).reshape(devices * slots, LANES)

    results = [None] * sections
    for section in reversed(range(sections)):
        low, high = edges(held, 0, SUB)
        forcing = spread_forcing(
            ids, received, section, sections, slots, (rows, share, nlon)
        )
        held = sweep(held, low, high, coeff, coeff_low, coeff_high, forcing, section)
        results[section] = held
    mine = lax.all_to_all(jnp.stack(results), "tm", 0, 1)
    return mine.reshape(1, rows, levels, nlon).astype(F32)


def solution(mesh):
    in_specs = (
        P("tm", "lat", None, None),
        P("tm", "lat", None, None),
        P("lat", None, None),
        P(("tm", "lat"), None, None),
        P(("tm", "lat"), None),
        P(("tm", "lat"), None),
        P(("tm", "lat"), None),
        P(("tm", "lat"), None),
        P(("tm", "lat")),
    )
    out_specs = P("tm", "lat", None, None)
    return jax.shard_map(
        per_device, mesh=mesh, in_specs=in_specs, out_specs=out_specs, check_vma=False
    )
```

time: 392 us -> 185 us (0.47); the launches traced: 394 us -> 183 us
  waiting for transfers between devices: 176 us -> 27.7 us
  other arithmetic: 66.2 us -> 7.07 us
  Pallas kernels: 0 us -> 56.9 us
  local copies, waits for them, and re-layouts: 57.3 us -> 16.6 us
  starting transfers between devices: 86 us -> 49.1 us
  blocking collectives: 0 us -> 25.6 us
  matrix products: 7.49 us -> 0 us
    ppermute x20 -> x10, waiting for transfers between devices: 164 us -> 18.1 us  [the longest x5 16.1 us: edges(): lax.ppermute(lax.slice_in_dim(block, size - width, size, axis=dim), 'lat'...]
    pallas_call x0 -> x11, Pallas kernels: none -> 56.9 us  [the longest x4 27.6 us: spread_forcing(): pl.pallas_call(body, name=f'spread_forcing_{section}', in_specs=[SMEM, VM...]
    add x4 -> x0, other arithmetic: 44.3 us -> none  [advance(): return forcing + propagate(incoming, coeff_own)]
    ppermute x20 -> x10, starting transfers between devices: 69.8 us -> 33.7 us  [the longest x5 22.6 us: edges(): lax.ppermute(lax.slice_in_dim(block, 0, width, axis=dim), 'lat', backward)]
    all_to_all x0 -> x2, blocking collectives: none -> 25.6 us  [the longest x1 15.9 us: per_device(): mine = lax.all_to_all(jnp.stack(results), 'tm', 0, 1)]
    transpose x2 -> x0, local copies, waits for them, and re-layouts: 13.3 us -> none  [the longest x1 6.69 us: per_device(): states = traj.reshape(lat_dev, levels, per_row, TW).transpose(0, 2, 1, 3)...]
    mul x9 -> x0, other arithmetic: 8.37 us -> none  [the longest x8 8.35 us: propagate(): weighted = coeffs * field]
    dot_general x2 -> x0, matrix products: 7.49 us -> none  [the longest x1 4.95 us: block_terms(): jnp.einsum('bct,bt->bc', jac_f, state, precision=lax.Precision.HIGHEST)]
  transfers between devices with their start and end apart: 23 -> 13, of which waited for: 22 -> 4; matrix products, arithmetic and copies ran while one was open for 6% -> 4% of each run, Pallas kernels for 0% -> 15%
where the time goes in v1:
time: 185 us; the launch traced here: 183 us
  Pallas kernels  56.9 us (31%)
  starting transfers between devices  49.1 us (27%)
  waiting for transfers between devices  27.7 us (15%)
  blocking collectives  25.6 us (14%)
  local copies, waits for them, and re-layouts  16.6 us (9%)
  other arithmetic  7.07 us (4%)
    pallas_call x4, Pallas kernels, spread_forcing(): pl.pallas_call(body, name=f'spread_forcing_{section}', in_specs=[SMEM, VM...  27.6 us
    ppermute x5, starting transfers between devices, edges(): lax.ppermute(lax.slice_in_dim(block, 0, width, axis=dim), 'lat', backward)  22.6 us
    ppermute x5, waiting for transfers between devices, edges(): lax.ppermute(lax.slice_in_dim(block, size - width, size, axis=dim), 'lat'...  16.1 us
    all_to_all x1, blocking collectives, per_device(): mine = lax.all_to_all(jnp.stack(results), 'tm', 0, 1)  15.9 us
    pallas_call x4, Pallas kernels, sweep(): pl.pallas_call(body, name=f'sweep_{section}', grid=(1,), in_specs=[full(h...  12.4 us
    ppermute x5, starting transfers between devices, edges(): lax.ppermute(lax.slice_in_dim(block, size - width, size, axis=dim), 'lat'...  11.1 us
    all_to_all x2, starting transfers between devices, exchange(): return lax.all_to_all(x, every, split_axis=0, concat_axis=0, tiled=True)  10.4 us
    all_to_all x1, blocking collectives, exchange(): return lax.all_to_all(x, every, split_axis=0, concat_axis=0, tiled=True)  9.75 us
  transfers between devices with their start and end apart: 13, of which 4 were waited for; matrix products, arithmetic and copies ran while one was open for 4% of the time, Pallas kernels for 15%

profile of v1, /device:TPU:12, one launch (start us, length us, event | category | flops | bytes accessed | tf_op | source)
XLA Modules:
  0.0 183.2 jit_solution(18277309527510294887)
XLA Ops:
  0.0 3.4 %route.1 = (s32[96]{0:T(128)}, s32[768]{0:T(1024)}) custom-call(s32[96]{0:T(128)} %bitcast.32, s32[96]{0:T(128)} %tile_ref.1), custom_call_target="tpu_custom_call" | custom-call | tf_op jit(solution)/shard_map/route/pallas_call | solution.py:47
  3.4 1.4 all_to_all.33
  4.8 6.0 %all-to-all-start.1 = ((s32[32,1,24]{2,1,0:T(1,128)}), s32[32,1,24]{2,1,0:T(1,128)S(1)}, u32[]{:S(2)}, u32[]{:S(2)}) async-start(s32[32,1,24]{2,1,0:T(1,128)} %bitcast.7), calls=%async_computation.1 | async-start | bytes 32768 | tf_op jit(solution)/shard_map/all_to_all | solution.py:343
  10.8 5.0 %all-to-all-done.1 = s32[32,1,24]{2,1,0:T(1,128)S(1)} async-done(((s32[32,1,24]{2,1,0:T(1,128)}), s32[32,1,24]{2,1,0:T(1,128)S(1)}, u32[]{:S(2)}, u32[]{:S(2)}) %all-to-all-start.1) | async-done | bytes 3104 | tf_op jit(solution)/shard_map/all_to_all | solution.py:343
  15.7 0.5 broadcast.3
  16.2 0.7 reduce.3
  16.9 0.7 reshape.56.ids_ref
  17.6 8.0 %fetch_states.1 = f32[192,128]{1,0:T(8,128)} custom-call(s32[1]{0:T(128)} %bitcast.8.place_ref, s32[768]{0:T(1024)} %reshape.56.ids_ref, f32[4,64,2048]{2,1,0:T(8,128)} %bitcast.30), custom_call_target="tpu_custom_call" | custom-call | tf_op jit(solution)/shard_map/fetch_states/pallas_call | solution.py:102
  25.6 0.9 reshape.58
  26.5 9.7 %all_to_all.43 = f32[32,6,128]{2,1,0:T(8,128)S(1)} all-to-all(f32[32,6,128]{2,1,0:T(8,128)S(1)} %reshape.58), channel_id=1, replica_groups=mesh['tm'=4,'lat'=8] {'tm','lat'}, dimensions={0} | all-to-all | bytes 196608 | tf_op jit(solution)/shard_map/all_to_all | solution.py:343
  36.3 0.7 reshape.59.found_ref
  36.9 5.5 %block_terms.1 = f32[192,128]{1,0:T(8,128)} custom-call(s32[96]{0:T(128)} %get-tuple-element.8.slot_ref, bf16[96,128,128]{2,1,0:T(8,128)(2,1)} %jac_ref.1, f32[192,128]{1,0:T(8,128)} %reshape.59.found_ref, f32[96,128]{1,0:T(8,128)} %value_ref.1, f32[96,128]{1,0:T(8,128)} %weight_ref.1, s32[96,128]{1,0:T(8,128)} %valid_ref.1), custom_call_target="tpu_custom_call" | custom-call | tf_op jit(solution)/shard_map/block_terms/pallas_call | solution.py:184
  42.4 1.6 reshape.60
  44.0 4.4 %all-to-all-start.3 = ((f32[32,6,128]{2,1,0:T(8,128)}), f32[32,6,128]{2,1,0:T(8,128)S(1)}, u32[]{:S(2)}, u32[]{:S(2)}) async-start(f32[32,6,128]{2,1,0:T(8,128)} %reshape.60), calls=%async_computation.3 | async-start | bytes 262144 | tf_op jit(solution)/shard_map/all_to_all | solution.py:343
  48.4 0.1 convert_element_type.42
  48.5 0.0 copy-start.4
  48.6 1.2 copy.12
  49.7 4.7 %all-to-all-done.3 = f32[32,6,128]{2,1,0:T(8,128)S(1)} async-done(((f32[32,6,128]{2,1,0:T(8,128)}), f32[32,6,128]{2,1,0:T(8,128)S(1)}, u32[]{:S(2)}, u32[]{:S(2)}) %all-to-all-start.3) | async-done | bytes 98336 | tf_op jit(solution)/shard_map/all_to_all | solution.py:343
  54.4 5.0 %all-to-all-start = ((f16[1,4,4,16,2048]{4,3,1,0,2:T(8,128)(2,1)}), f16[1,4,4,16,2048]{4,3,1,0,2:T(8,128)(2,1)S(1)}, u32[]{:S(2)}, u32[]{:S(2)}) async-start(f16[1,4,4,16,2048]{4,3,1,0,2:T(8,128)(2,1)} %copy.12), calls=%async_computation | async-start | bytes 2097152 | tf_op jit(solution)/shard_map/all_to_all | solution.py:345
  59.4 2.9 %collective-permute-start = (bf16[2,16,2048]{2,1,0:T(8,128)(2,1)S(1)}, bf16[2,16,2048]{2,1,0:T(8,128)(2,1)S(1)}, u32[]{:S(2)}, u32[]{:S(2)}) collective-permute-start(bf16[2,16,2048]{2,1,0:T(8,128)(2,1)S(1)} %get-tuple-element.12), channel_id=1, source_target_pairs={{0,1},{1,2},{2,3},{3,4},{4,5},{5,6},{6,7},{8,9},{9,10},{10,11},{11... | collective-permute-start | bytes 393224 | tf_op jit(solution)/shard_map/ppermute | solution.py:315
  62.3 3.8 %collective-permute-start.1 = (bf16[2,16,2048]{2,1,0:T(8,128)(2,1)S(1)}, bf16[2,16,2048]{2,1,0:T(8,128)(2,1)S(1)}, u32[]{:S(2)}, u32[]{:S(2)}) collective-permute-start(bf16[2,16,2048]{2,1,0:T(8,128)(2,1)S(1)} %get-tuple-element.11), channel_id=1, source_target_pairs={{1,0},{2,1},{3,2},{4,3},{5,4},{6,5},{7,6},{9,8},{10,9},{11,10},{12... | collective-permute-start | bytes 393224 | tf_op jit(solution)/shard_map/ppermute | solution.py:316
  66.1 0.7 constant_dynamic-slice_fusion.2.held_ref
  66.9 0.7 reshape.61.recv_ref
  67.5 6.9 %spread_forcing_3.1.f_ref = f32[4,16,2048]{2,1,0:T(8,128)} custom-call(s32[768]{0:T(1024)} %reshape.56.ids_ref, f32[192,128]{1,0:T(8,128)} %reshape.61.recv_ref), custom_call_target="tpu_custom_call" | custom-call | tf_op jit(solution)/shard_map/spread_forcing_3/pallas_call | solution.py:246
  74.4 0.0 all-to-all-done
  74.4 0.2 fusion
  74.6 2.0 %collective-permute-start.2 = (f16[4,2,16,2048]{3,2,1,0:T(8,128)(2,1)S(1)}, f16[4,2,16,2048]{3,2,1,0:T(8,128)(2,1)S(1)}, u32[]{:S(2)}, u32[]{:S(2)}) collective-permute-start(f16[4,2,16,2048]{3,2,1,0:T(8,128)(2,1)S(1)} %get-tuple-element.10), channel_id=1, source_target_pairs={{0,1},{1,2},{2,3},{3,4},{4,5},{5,6},{6,7},{8,9},{9,10},{10,11},{11... | collective-permute-start | bytes 1572872 | tf_op jit(solution)/shard_map/ppermute | solution.py:315
  76.6 4.7 %collective-permute-start.3 = (f16[4,2,16,2048]{3,2,1,0:T(8,128)(2,1)S(1)}, f16[4,2,16,2048]{3,2,1,0:T(8,128)(2,1)S(1)}, u32[]{:S(2)}, u32[]{:S(2)}) collective-permute-start(f16[4,2,16,2048]{3,2,1,0:T(8,128)(2,1)S(1)} %get-tuple-element.9), channel_id=1, source_target_pairs={{1,0},{2,1},{3,2},{4,3},{5,4},{6,5},{7,6},{9,8},{10,9},{11,10},{12... | collective-permute-start | bytes 1572872 | tf_op jit(solution)/shard_map/ppermute | solution.py:316
  81.4 1.5 bitcast_convert_fusion.1.c_ref
  82.9 16.1 %collective-permute-done.2 = f16[4,2,16,2048]{3,2,1,0:T(8,128)(2,1)S(1)} collective-permute-done((f16[4,2,16,2048]{3,2,1,0:T(8,128)(2,1)S(1)}, f16[4,2,16,2048]{3,2,1,0:T(8,128)(2,1)S(1)}, u32[]{:S(2)}, u32[]{:S(2)}) %collective-permute-start.2) | collective-permute-done | bytes 524320 | tf_op jit(solution)/shard_map/ppermute | solution.py:315
  99.0 1.1 convert_element_type.45.cl_ref
  100.0 2.0 %collective-permute-done.3 = f16[4,2,16,2048]{3,2,1,0:T(8,128)(2,1)S(1)} collective-permute-done((f16[4,2,16,2048]{3,2,1,0:T(8,128)(2,1)S(1)}, f16[4,2,16,2048]{3,2,1,0:T(8,128)(2,1)S(1)}, u32[]{:S(2)}, u32[]{:S(2)}) %collective-permute-start.3) | collective-permute-done | bytes 524320 | tf_op jit(solution)/shard_map/ppermute | solution.py:316
  102.1 1.1 convert_element_type.46.ch_ref
  103.1 0.0 collective-permute-done.low_ref
  103.1 0.0 collective-permute-done.1.high_ref
  103.1 0.7 copy-done.5
  103.8 0.6 copy-done.6
  104.4 3.1 %sweep_3.1.held_ref = bf16[4,16,2048]{2,1,0:T(8,128)(2,1)} custom-call(bf16[4,16,2048]{2,1,0:T(8,128)(2,1)} %constant_dynamic-slice_fusion.2.held_ref, bf16[2,16,2048]{2,1,0:T(8,128)(2,1)} %copy-done.5, bf16[2,16,2048]{2,1,0:T(8,128)(2,1)} %copy-done.6, f32[4,4,16,2048]{3,2,1,0:T(8,128)} %bitcast_convert_fusion.1.c_ref, ...), custom_call_target="tpu_custom_call" | custom-call | tf_op jit(solution)/shard_map/sweep_3/pallas_call | solution.py:296
  107.5 1.0 fusion.3
  108.5 2.4 %collective-permute-start.4 = (bf16[2,16,2048]{2,1,0:T(8,128)(2,1)S(1)}, bf16[2,16,2048]{2,1,0:T(8,128)(2,1)S(1)}, u32[]{:S(2)}, u32[]{:S(2)}) collective-permute-start(bf16[2,16,2048]{2,1,0:T(8,128)(2,1)S(1)} %get-tuple-element.18), channel_id=1, source_target_pairs={{0,1},{1,2},{2,3},{3,4},{4,5},{5,6},{6,7},{8,9},{9,10},{10,11},{11... | collective-permute-start | bytes 393224 | tf_op jit(solution)/shard_map/ppermute | solution.py:315
  110.9 4.4 %collective-permute-start.5 = (bf16[2,16,2048]{2,1,0:T(8,128)(2,1)S(1)}, bf16[2,16,2048]{2,1,0:T(8,128)(2,1)S(1)}, u32[]{:S(2)}, u32[]{:S(2)}) collective-permute-start(bf16[2,16,2048]{2,1,0:T(8,128)(2,1)S(1)} %get-tuple-element.17), channel_id=1, source_target_pairs={{1,0},{2,1},{3,2},{4,3},{5,4},{6,5},{7,6},{9,8},{10,9},{11,10},{12... | collective-permute-start | bytes 393224 | tf_op jit(solution)/shard_map/ppermute | solution.py:316
  115.3 6.9 %spread_forcing_2.1.f_ref = f32[4,16,2048]{2,1,0:T(8,128)} custom-call(s32[768]{0:T(1024)} %reshape.56.ids_ref, f32[192,128]{1,0:T(8,128)} %reshape.61.recv_ref), custom_call_target="tpu_custom_call" | custom-call | tf_op jit(solution)/shard_map/spread_forcing_2/pallas_call | solution.py:246
  122.2 0.7 copy-done.9
  122.9 0.6 copy-done.11
  123.5 3.1 %sweep_2.1.held_ref = bf16[4,16,2048]{2,1,0:T(8,128)(2,1)} custom-call(bf16[4,16,2048]{2,1,0:T(8,128)(2,1)} %sweep_3.1.held_ref, bf16[2,16,2048]{2,1,0:T(8,128)(2,1)} %copy-done.9, bf16[2,16,2048]{2,1,0:T(8,128)(2,1)} %copy-done.11, f32[4,4,16,2048]{3,2,1,0:T(8,128)} %bitcast_convert_fusion.1.c_ref, f32[4,2,16,2048]{3,2,1,0:T(8,128)} %convert_element_type.45.cl_ref, ...), custom_call_target="tpu_custom_call" | custom-call | tf_op jit(solution)/shard_map/sweep_2/pallas_call | solution.py:296
  126.6 1.0 fusion.2
  127.6 1.9 %collective-permute-start.6 = (bf16[2,16,2048]{2,1,0:T(8,128)(2,1)S(1)}, bf16[2,16,2048]{2,1,0:T(8,128)(2,1)S(1)}, u32[]{:S(2)}, u32[]{:S(2)}) collective-permute-start(bf16[2,16,2048]{2,1,0:T(8,128)(2,1)S(1)} %get-tuple-element.16), channel_id=1, source_target_pairs={{0,1},{1,2},{2,3},{3,4},{4,5},{5,6},{6,7},{8,9},{9,10},{10,11},{11... | collective-permute-start | bytes 393224 | tf_op jit(solution)/shard_map/ppermute | solution.py:315
  129.5 4.8 %collective-permute-start.7 = (bf16[2,16,2048]{2,1,0:T(8,128)(2,1)S(1)}, bf16[2,16,2048]{2,1,0:T(8,128)(2,1)S(1)}, u32[]{:S(2)}, u32[]{:S(2)}) collective-permute-start(bf16[2,16,2048]{2,1,0:T(8,128)(2,1)S(1)} %get-tuple-element.15), channel_id=1, source_target_pairs={{1,0},{2,1},{3,2},{4,3},{5,4},{6,5},{7,6},{9,8},{10,9},{11,10},{12... | collective-permute-start | bytes 393224 | tf_op jit(solution)/shard_map/ppermute | solution.py:316
  134.4 6.9 %spread_forcing_1.1.f_ref = f32[4,16,2048]{2,1,0:T(8,128)} custom-call(s32[768]{0:T(1024)} %reshape.56.ids_ref, f32[192,128]{1,0:T(8,128)} %reshape.61.recv_ref), custom_call_target="tpu_custom_call" | custom-call | tf_op jit(solution)/shard_map/spread_forcing_1/pallas_call | solution.py:246
  141.3 0.0 collective-permute-done.7.high_ref
  141.3 0.6 copy-done.10
  141.9 0.7 copy-done.12
  142.6 3.1 %sweep_1.1.held_ref = bf16[4,16,2048]{2,1,0:T(8,128)(2,1)} custom-call(bf16[4,16,2048]{2,1,0:T(8,128)(2,1)} %sweep_2.1.held_ref, bf16[2,16,2048]{2,1,0:T(8,128)(2,1)} %copy-done.10, bf16[2,16,2048]{2,1,0:T(8,128)(2,1)} %copy-done.12, f32[4,4,16,2048]{3,2,1,0:T(8,128)} %bitcast_convert_fusion.1.c_ref, f32[4,2,16,2048]{3,2,1,0:T(8,128)} %convert_element_type.45.cl_ref, ...), custom_call_target="tpu_custom_call" | custom-call | tf_op jit(solution)/shard_map/sweep_1/pallas_call | solution.py:296
  145.7 1.0 fusion.1
  146.6 1.9 %collective-permute-start.8 = (bf16[2,16,2048]{2,1,0:T(8,128)(2,1)S(1)}, bf16[2,16,2048]{2,1,0:T(8,128)(2,1)S(1)}, u32[]{:S(2)}, u32[]{:S(2)}) collective-permute-start(bf16[2,16,2048]{2,1,0:T(8,128)(2,1)S(1)} %get-tuple-element.14), channel_id=1, source_target_pairs={{0,1},{1,2},{2,3},{3,4},{4,5},{5,6},{6,7},{8,9},{9,10},{10,11},{11... | collective-permute-start | bytes 393224 | tf_op jit(solution)/shard_map/ppermute | solution.py:315
  148.6 4.8 %collective-permute-start.9 = (bf16[2,16,2048]{2,1,0:T(8,128)(2,1)S(1)}, bf16[2,16,2048]{2,1,0:T(8,128)(2,1)S(1)}, u32[]{:S(2)}, u32[]{:S(2)}) collective-permute-start(bf16[2,16,2048]{2,1,0:T(8,128)(2,1)S(1)} %get-tuple-element.13), channel_id=1, source_target_pairs={{1,0},{2,1},{3,2},{4,3},{5,4},{6,5},{7,6},{9,8},{10,9},{11,10},{12... | collective-permute-start | bytes 393224 | tf_op jit(solution)/shard_map/ppermute | solution.py:316
  153.4 6.8 %spread_forcing_0.1.f_ref = f32[4,16,2048]{2,1,0:T(8,128)} custom-call(s32[768]{0:T(1024)} %reshape.56.ids_ref, f32[192,128]{1,0:T(8,128)} %reshape.61.recv_ref), custom_call_target="tpu_custom_call" | custom-call | tf_op jit(solution)/shard_map/spread_forcing_0/pallas_call | solution.py:246
  160.3 0.0 collective-permute-done.9.high_ref
  160.3 0.6 copy-done.7
  160.9 0.6 copy-done.8
  161.6 3.1 %sweep_0.1 = bf16[4,16,2048]{2,1,0:T(8,128)(2,1)} custom-call(bf16[4,16,2048]{2,1,0:T(8,128)(2,1)} %sweep_1.1.held_ref, bf16[2,16,2048]{2,1,0:T(8,128)(2,1)} %copy-done.7, bf16[2,16,2048]{2,1,0:T(8,128)(2,1)} %copy-done.8, f32[4,4,16,2048]{3,2,1,0:T(8,128)} %bitcast_convert_fusion.1.c_ref, f32[4,2,16,2048]{3,2,1,0:T(8,128)} %convert_element_type.45.cl_ref, ...), custom_call_target="tpu_custom_call" | custom-call | tf_op jit(solution)/shard_map/sweep_0/pallas_call | solution.py:296
  164.7 1.1 maximum_bitcast_fusion
  165.8 15.9 %all_to_all.44 = bf16[4,4,1,16,2048]{4,3,1,2,0:T(8,128)(2,1)S(1)} all-to-all(bf16[4,4,1,16,2048]{4,3,1,2,0:T(8,128)(2,1)S(1)} %maximum_bitcast_fusion), channel_id=1, replica_groups=mesh['tm'=4,'lat'=8] {'tm'}, dimensions={0} | all-to-all | bytes 2097152 | tf_op jit(solution)/shard_map/all_to_all | solution.py:369
  181.7 1.6 bitcast_convert_fusion
  (22 shorter events, 0.1 us)
Async XLA Ops:
  4.8 11.0 %all-to-all-start.1 = ((s32[32,1,24]{2,1,0:T(1,128)}), s32[32,1,24]{2,1,0:T(1,128)S(1)}, u32[]{:S(2)}, u32[]{:S(2)}) async-start(s32[32,1,24]{2,1,0:T(1,128)} %bitcast.7), calls=%async_computation.1 | async-start | bytes 32768 | tf_op jit(solution)/shard_map/all_to_all | solution.py:343
  36.3 12.1 %copy-start.3 = (f32[1,4,64,2048]{3,2,1,0:T(8,128)S(1)}, f32[1,4,64,2048]{3,2,1,0:T(8,128)}, u32[]{:S(2)}) copy-start(f32[1,4,64,2048]{3,2,1,0:T(8,128)} %param.10) | copy-start | bytes 6291460
  44.0 10.4 %all-to-all-start.3 = ((f32[32,6,128]{2,1,0:T(8,128)}), f32[32,6,128]{2,1,0:T(8,128)S(1)}, u32[]{:S(2)}, u32[]{:S(2)}) async-start(f32[32,6,128]{2,1,0:T(8,128)} %reshape.60), calls=%async_computation.3 | async-start | bytes 262144 | tf_op jit(solution)/shard_map/all_to_all | solution.py:343
  48.5 10.8 %copy-start.4 = (bf16[4,64,2048]{2,1,0:T(8,128)(2,1)S(1)}, bf16[4,64,2048]{2,1,0:T(8,128)(2,1)}, u32[]{:S(2)}) copy-start(bf16[4,64,2048]{2,1,0:T(8,128)(2,1)} %param.11) | copy-start | bytes 3145732
  54.4 20.1 %all-to-all-start = ((f16[1,4,4,16,2048]{4,3,1,0,2:T(8,128)(2,1)}), f16[1,4,4,16,2048]{4,3,1,0,2:T(8,128)(2,1)S(1)}, u32[]{:S(2)}, u32[]{:S(2)}) async-start(f16[1,4,4,16,2048]{4,3,1,0,2:T(8,128)(2,1)} %copy.12), calls=%async_computation | async-start | bytes 2097152 | tf_op jit(solution)/shard_map/all_to_all | solution.py:345
  59.4 43.8 %collective-permute-start = (bf16[2,16,2048]{2,1,0:T(8,128)(2,1)S(1)}, bf16[2,16,2048]{2,1,0:T(8,128)(2,1)S(1)}, u32[]{:S(2)}, u32[]{:S(2)}) collective-permute-start(bf16[2,16,2048]{2,1,0:T(8,128)(2,1)S(1)} %get-tuple-element.12), channel_id=1, source_target_pairs={{0,1},{1,2},{2,3},{3,4},{4,5},{5,6},{6,7},{8,9},{9,10},{10,11},{11... | collective-permute-start | bytes 393224 | tf_op jit(solution)/shard_map/ppermute | solution.py:315
  62.3 40.9 %collective-permute-start.1 = (bf16[2,16,2048]{2,1,0:T(8,128)(2,1)S(1)}, bf16[2,16,2048]{2,1,0:T(8,128)(2,1)S(1)}, u32[]{:S(2)}, u32[]{:S(2)}) collective-permute-start(bf16[2,16,2048]{2,1,0:T(8,128)(2,1)S(1)} %get-tuple-element.11), channel_id=1, source_target_pairs={{1,0},{2,1},{3,2},{4,3},{5,4},{6,5},{7,6},{9,8},{10,9},{11,10},{12... | collective-permute-start | bytes 393224 | tf_op jit(solution)/shard_map/ppermute | solution.py:316
  74.6 24.3 %collective-permute-start.2 = (f16[4,2,16,2048]{3,2,1,0:T(8,128)(2,1)S(1)}, f16[4,2,16,2048]{3,2,1,0:T(8,128)(2,1)S(1)}, u32[]{:S(2)}, u32[]{:S(2)}) collective-permute-start(f16[4,2,16,2048]{3,2,1,0:T(8,128)(2,1)S(1)} %get-tuple-element.10), channel_id=1, source_target_pairs={{0,1},{1,2},{2,3},{3,4},{4,5},{5,6},{6,7},{8,9},{9,10},{10,11},{11... | collective-permute-start | bytes 1572872 | tf_op jit(solution)/shard_map/ppermute | solution.py:315
  76.6 25.4 %collective-permute-start.3 = (f16[4,2,16,2048]{3,2,1,0:T(8,128)(2,1)S(1)}, f16[4,2,16,2048]{3,2,1,0:T(8,128)(2,1)S(1)}, u32[]{:S(2)}, u32[]{:S(2)}) collective-permute-start(f16[4,2,16,2048]{3,2,1,0:T(8,128)(2,1)S(1)} %get-tuple-element.9), channel_id=1, source_target_pairs={{1,0},{2,1},{3,2},{4,3},{5,4},{6,5},{7,6},{9,8},{10,9},{11,10},{12... | collective-permute-start | bytes 1572872 | tf_op jit(solution)/shard_map/ppermute | solution.py:316
  103.1 0.7 copy-start.5
  103.8 0.6 copy-start.6
  108.5 13.7 %collective-permute-start.4 = (bf16[2,16,2048]{2,1,0:T(8,128)(2,1)S(1)}, bf16[2,16,2048]{2,1,0:T(8,128)(2,1)S(1)}, u32[]{:S(2)}, u32[]{:S(2)}) collective-permute-start(bf16[2,16,2048]{2,1,0:T(8,128)(2,1)S(1)} %get-tuple-element.18), channel_id=1, source_target_pairs={{0,1},{1,2},{2,3},{3,4},{4,5},{5,6},{6,7},{8,9},{9,10},{10,11},{11... | collective-permute-start | bytes 393224 | tf_op jit(solution)/shard_map/ppermute | solution.py:315
  110.9 11.3 %collective-permute-start.5 = (bf16[2,16,2048]{2,1,0:T(8,128)(2,1)S(1)}, bf16[2,16,2048]{2,1,0:T(8,128)(2,1)S(1)}, u32[]{:S(2)}, u32[]{:S(2)}) collective-permute-start(bf16[2,16,2048]{2,1,0:T(8,128)(2,1)S(1)} %get-tuple-element.17), channel_id=1, source_target_pairs={{1,0},{2,1},{3,2},{4,3},{5,4},{6,5},{7,6},{9,8},{10,9},{11,10},{12... | collective-permute-start | bytes 393224 | tf_op jit(solution)/shard_map/ppermute | solution.py:316
  122.2 0.7 copy-start.9
  122.9 0.6 copy-start.11
  127.6 13.7 %collective-permute-start.6 = (bf16[2,16,2048]{2,1,0:T(8,128)(2,1)S(1)}, bf16[2,16,2048]{2,1,0:T(8,128)(2,1)S(1)}, u32[]{:S(2)}, u32[]{:S(2)}) collective-permute-start(bf16[2,16,2048]{2,1,0:T(8,128)(2,1)S(1)} %get-tuple-element.16), channel_id=1, source_target_pairs={{0,1},{1,2},{2,3},{3,4},{4,5},{5,6},{6,7},{8,9},{9,10},{10,11},{11... | collective-permute-start | bytes 393224 | tf_op jit(solution)/shard_map/ppermute | solution.py:315
  129.5 11.7 %collective-permute-start.7 = (bf16[2,16,2048]{2,1,0:T(8,128)(2,1)S(1)}, bf16[2,16,2048]{2,1,0:T(8,128)(2,1)S(1)}, u32[]{:S(2)}, u32[]{:S(2)}) collective-permute-start(bf16[2,16,2048]{2,1,0:T(8,128)(2,1)S(1)} %get-tuple-element.15), channel_id=1, source_target_pairs={{1,0},{2,1},{3,2},{4,3},{5,4},{6,5},{7,6},{9,8},{10,9},{11,10},{12... | collective-permute-start | bytes 393224 | tf_op jit(solution)/shard_map/ppermute | solution.py:316
  141.3 0.6 copy-start.10
  141.9 0.7 copy-start.12
  146.6 13.6 %collective-permute-start.8 = (bf16[2,16,2048]{2,1,0:T(8,128)(2,1)S(1)}, bf16[2,16,2048]{2,1,0:T(8,128)(2,1)S(1)}, u32[]{:S(2)}, u32[]{:S(2)}) collective-permute-start(bf16[2,16,2048]{2,1,0:T(8,128)(2,1)S(1)} %get-tuple-element.14), channel_id=1, source_target_pairs={{0,1},{1,2},{2,3},{3,4},{4,5},{5,6},{6,7},{8,9},{9,10},{10,11},{11... | collective-permute-start | bytes 393224 | tf_op jit(solution)/shard_map/ppermute | solution.py:315
  148.6 11.7 %collective-permute-start.9 = (bf16[2,16,2048]{2,1,0:T(8,128)(2,1)S(1)}, bf16[2,16,2048]{2,1,0:T(8,128)(2,1)S(1)}, u32[]{:S(2)}, u32[]{:S(2)}) collective-permute-start(bf16[2,16,2048]{2,1,0:T(8,128)(2,1)S(1)} %get-tuple-element.13), channel_id=1, source_target_pairs={{1,0},{2,1},{3,2},{4,3},{5,4},{6,5},{7,6},{9,8},{10,9},{11,10},{12... | collective-permute-start | bytes 393224 | tf_op jit(solution)/shard_map/ppermute | solution.py:316
  160.2 4.4 %copy-start = (bf16[4,16,2048]{2,1,0:T(8,128)(2,1)S(1)}, bf16[4,16,2048]{2,1,0:T(8,128)(2,1)}, u32[]{:S(2)}) copy-start(bf16[4,16,2048]{2,1,0:T(8,128)(2,1)} %sweep_3.1.held_ref) | copy-start | bytes 786436
  160.3 4.4 %copy-start.1 = (bf16[4,16,2048]{2,1,0:T(8,128)(2,1)S(1)}, bf16[4,16,2048]{2,1,0:T(8,128)(2,1)}, u32[]{:S(2)}) copy-start(bf16[4,16,2048]{2,1,0:T(8,128)(2,1)} %sweep_2.1.held_ref) | copy-start | bytes 786436
  160.3 4.4 %copy-start.2 = (bf16[4,16,2048]{2,1,0:T(8,128)(2,1)S(1)}, bf16[4,16,2048]{2,1,0:T(8,128)(2,1)}, u32[]{:S(2)}) copy-start(bf16[4,16,2048]{2,1,0:T(8,128)(2,1)} %sweep_1.1.held_ref) | copy-start | bytes 786436
  160.3 0.7 copy-start.7
  160.9 0.6 copy-start.8

commit v2 on v1

--- a/solution.py
+++ b/solution.py
@@ -16,6 +16,12 @@
 VMEM = pl.BlockSpec(memory_space=pltpu.VMEM)
 
 
+def split_index(x, n):
+    if n & (n - 1):
+        return x // n, x % n
+    return lax.shift_right_logical(x, n.bit_length() - 1), lax.bitwise_and(x, n - 1)
+
+
 def route(owner, tile, sections, bands, slots):
     devices = sections * bands
     blocks = owner.shape[0]
@@ -35,11 +41,11 @@
             rank = used_ref[target]
             used_ref[target] = rank + 1
             slot_ref[k] = target * slots + rank
-            section = target // bands
-            band = target % bands
+            section, band = split_index(target, bands)
+            tile = tile_ref[k]
             for other in range(sections):
                 at = ((other * bands + band) * sections + section) * slots + rank
-                table_ref[at] = tile_ref[k]
+                table_ref[at] = tile
             return c
 
         lax.fori_loop(0, blocks, put, 0)
@@ -63,6 +69,8 @@
     pairs = LANES // TW
     per_target = sections * slots
     count = ids.shape[0] // sections
+    devices = count // slots
+    run = min(devices, pairs)
 
     def body(place_ref, ids_ref, traj_ref, out_ref, pairs_ref):
         lane = lax.broadcasted_iota(jnp.int32, (levels, LANES), 1)
@@ -73,18 +81,17 @@
         for group in range(count // pairs):
 
             def one(k, gathered):
-                i = group * pairs + k
-                at = (i // slots) * per_target + mine + i % slots
-                tile = jnp.maximum(ids_ref[at], 0)
-                row = tile // per_row
-                column = tile % per_row
-                start = pl.multiple_of(column // pairs * LANES, LANES)
-                shift = (TW * k + LANES - column % pairs * TW) % LANES
+                slot, device = split_index(group * pairs + k, devices)
+                tile = jnp.maximum(ids_ref[device * per_target + mine + slot], 0)
+                row, column = split_index(tile, per_row)
+                block, off = split_index(column, pairs)
+                start = pl.multiple_of(block * LANES, LANES)
+                shift = lax.bitwise_and(TW * (k + pairs - off), LANES - 1)
                 turned = pltpu.roll(traj_ref[row, :, pl.ds(start, LANES)], shift, 1)
                 return jnp.where(lane // TW == k, turned, gathered)
 
             gathered = lax.fori_loop(
-                0, pairs, one, jnp.zeros((levels, LANES), F32), unroll=8
+                0, pairs, one, jnp.zeros((levels, LANES), F32), unroll=16
             )
             pairs_ref[...] = sum(
                 lax.dot_general(
@@ -95,9 +102,12 @@
             )
             even = pairs_ref[pl.ds(0, pairs, stride=TW), :]
             odd = pairs_ref[pl.ds(1, pairs, stride=TW), :]
-            out_ref[group * pairs : (group + 1) * pairs, :] = jnp.where(
-                lane[:pairs] % TW == 0, even, odd
-            )
+            both = jnp.where(lane[:pairs] % TW == 0, even, odd)
+            for j in range(pairs // run):
+                slot, device = divmod(group * pairs + j * run, devices)
+                out_ref[pl.ds(device * slots + slot, run, stride=slots), :] = both[
+                    j * run : (j + 1) * run
+                ]
 
     return pl.pallas_call(
         body,
@@ -207,8 +217,12 @@
     count = received.shape[0]
     first = section * (LANES // sections)
 
-    def body(ids_ref, recv_ref, out_ref, pairs_ref, terms_ref):
-        out_ref[...] = jnp.zeros_like(out_ref)
+    heaps = min(slots, 3)
+
+    def body(ids_ref, recv_ref, out_ref, pairs_ref, terms_ref, *heap_refs):
+        heap_refs = (out_ref,) + heap_refs
+        for ref in heap_refs:
+            ref[...] = jnp.zeros_like(ref)
         lane = lax.broadcasted_iota(jnp.int32, (share, LANES), 1)
         level = lax.broadcasted_iota(jnp.int32, (share, LANES), 0)
         pick = (lane // TW == level + first // TW).astype(BF16)
@@ -227,21 +241,24 @@
                 for piece in split3(pairs_ref[...])
             )
 
-        def one(i, c):
-            at = (i // slots) * per_target + section * slots + i % slots
-            tile = jnp.maximum(ids_ref[at], 0)
-            row = tile // per_row
-            column = tile % per_row
-            start = pl.multiple_of(column // pairs * LANES, LANES)
-            off = column % pairs
-            shift = (off + pairs - i % pairs) % pairs * TW
-            turned = pltpu.roll(terms_ref[i // pairs], shift, 1)
-            out_ref[row, :, pl.ds(start, LANES)] += jnp.where(
-                lane // TW == off, turned, 0.0
-            )
+        def one(device, c):
+            for slot in range(slots):
+                tile = jnp.maximum(
+                    ids_ref[device * per_target + section * slots + slot], 0
+                )
+                group, k = split_index(device * slots + slot, pairs)
+                row, column = split_index(tile, per_row)
+                at, off = split_index(column, pairs)
+                start = pl.multiple_of(at * LANES, LANES)
+                shift = lax.bitwise_and(off + pairs - k, pairs - 1) * TW
+                turned = pltpu.roll(terms_ref[group], shift, 1)
+                heap_refs[slot % heaps][row, :, pl.ds(start, LANES)] += jnp.where(
+                    lane // TW == off, turned, 0.0
+                )
             return c
 
-        lax.fori_loop(0, count, one, 0, unroll=8)
+        lax.fori_loop(0, count // slots, one, 0, unroll=2)
+        out_ref[...] = sum(ref[...] for ref in heap_refs[1:]) + out_ref[...]
 
     return pl.pallas_call(
         body,
@@ -252,7 +269,8 @@
         scratch_shapes=[
             pltpu.VMEM((LANES, LANES), F32),
             pltpu.VMEM((count // pairs, share, LANES), F32),
-        ],
+        ]
+        + [pltpu.VMEM(shape, F32)] * (heaps - 1),
     )(ids, received)
 
 

time: 185 us -> 173 us (0.935)
  Pallas kernels: 56.9 us -> 42.4 us
    pallas_call x4, Pallas kernels: 27.6 us -> 15.9 us  [spread_forcing(): pl.pallas_call(body, name=f'spread_forcing_{section}', in_specs=[SMEM, VM...]
    ppermute x5, starting transfers between devices: 11.1 us -> 14.4 us  [edges(): lax.ppermute(lax.slice_in_dim(block, size - width, size, axis=dim), 'lat'...]
    ppermute x5, starting transfers between devices: 22.6 us -> 19.3 us  [edges(): lax.ppermute(lax.slice_in_dim(block, 0, width, axis=dim), 'lat', backward)]
    pallas_call x1, Pallas kernels: 8 us -> 5.44 us  [fetch_states(): pl.pallas_call(body, name='fetch_states', in_specs=[SMEM, SMEM, VMEM], ou...]
  transfers between devices with their start and end apart: 13 -> 13, of which waited for: 4 -> 6; matrix products, arithmetic and copies ran while one was open for 4% -> 4% of each run, Pallas kernels for 15% -> 9%
where the time goes in v2:
time: 173 us; the launch traced here: 170 us
  starting transfers between devices  49.1 us (28%)
  Pallas kernels  42.4 us (25%)
  waiting for transfers between devices  29 us (17%)
  blocking collectives  26.2 us (15%)
  local copies, waits for them, and re-layouts  16.3 us (9%)
  other arithmetic  7.07 us (4%)
    ppermute x5, starting transfers between devices, edges(): lax.ppermute(lax.slice_in_dim(block, 0, width, axis=dim), 'lat', backward)  19.3 us
    ppermute x5, waiting for transfers between devices, edges(): lax.ppermute(lax.slice_in_dim(block, size - width, size, axis=dim), 'lat'...  17.1 us
    all_to_all x1, blocking collectives, per_device(): mine = lax.all_to_all(jnp.stack(results), 'tm', 0, 1)  16.5 us
    pallas_call x4, Pallas kernels, spread_forcing(): pl.pallas_call(body, name=f'spread_forcing_{section}', in_specs=[SMEM, VM...  15.9 us
    ppermute x5, starting transfers between devices, edges(): lax.ppermute(lax.slice_in_dim(block, size - width, size, axis=dim), 'lat'...  14.4 us
    pallas_call x4, Pallas kernels, sweep(): pl.pallas_call(body, name=f'sweep_{section}', grid=(1,), in_specs=[full(h...  12.4 us
    all_to_all x2, starting transfers between devices, exchange(): return lax.all_to_all(x, every, split_axis=0, concat_axis=0, tiled=True)  10.4 us
    all_to_all x1, blocking collectives, exchange(): return lax.all_to_all(x, every, split_axis=0, concat_axis=0, tiled=True)  9.75 us
  transfers between devices with their start and end apart: 13, of which 6 were waited for; matrix products, arithmetic and copies ran while one was open for 4% of the time, Pallas kernels for 9%

profile of v2, /device:TPU:12, one launch (start us, length us, event | category | flops | bytes accessed | tf_op | source)
XLA Modules:
  0.0 170.3 jit_solution(2438716123435856860)
XLA Ops:
  0.0 3.1 %route.1 = (s32[96]{0:T(128)}, s32[768]{0:T(1024)}) custom-call(s32[96]{0:T(128)} %bitcast.32, s32[96]{0:T(128)} %tile_ref.1), custom_call_target="tpu_custom_call" | custom-call | tf_op jit(solution)/shard_map/route/pallas_call | solution.py:53
  3.2 1.4 all_to_all.33
  4.5 6.0 %all-to-all-start.1 = ((s32[32,1,24]{2,1,0:T(1,128)}), s32[32,1,24]{2,1,0:T(1,128)S(1)}, u32[]{:S(2)}, u32[]{:S(2)}) async-start(s32[32,1,24]{2,1,0:T(1,128)} %bitcast.7), calls=%async_computation.1 | async-start | bytes 32768 | tf_op jit(solution)/shard_map/all_to_all | solution.py:361
  10.5 5.0 %all-to-all-done.1 = s32[32,1,24]{2,1,0:T(1,128)S(1)} async-done(((s32[32,1,24]{2,1,0:T(1,128)}), s32[32,1,24]{2,1,0:T(1,128)S(1)}, u32[]{:S(2)}, u32[]{:S(2)}) %all-to-all-start.1) | async-done | bytes 3104 | tf_op jit(solution)/shard_map/all_to_all | solution.py:361
  15.5 0.5 broadcast.3
  16.0 0.7 reduce.3
  16.7 0.7 reshape.56.ids_ref
  17.4 5.4 %fetch_states.1 = f32[192,128]{1,0:T(8,128)} custom-call(s32[1]{0:T(128)} %bitcast.8.place_ref, s32[768]{0:T(1024)} %reshape.56.ids_ref, f32[4,64,2048]{2,1,0:T(8,128)} %bitcast.30), custom_call_target="tpu_custom_call" | custom-call | tf_op jit(solution)/shard_map/fetch_states/pallas_call | solution.py:112
  22.8 0.9 reshape.58
  23.7 9.7 %all_to_all.43 = f32[32,6,128]{2,1,0:T(8,128)S(1)} all-to-all(f32[32,6,128]{2,1,0:T(8,128)S(1)} %reshape.58), channel_id=1, replica_groups=mesh['tm'=4,'lat'=8] {'tm','lat'}, dimensions={0} | all-to-all | bytes 196608 | tf_op jit(solution)/shard_map/all_to_all | solution.py:361
  33.5 0.7 reshape.59.found_ref
  34.1 5.5 %block_terms.1 = f32[192,128]{1,0:T(8,128)} custom-call(s32[96]{0:T(128)} %get-tuple-element.8.slot_ref, bf16[96,128,128]{2,1,0:T(8,128)(2,1)} %jac_ref.1, f32[192,128]{1,0:T(8,128)} %reshape.59.found_ref, f32[96,128]{1,0:T(8,128)} %value_ref.1, f32[96,128]{1,0:T(8,128)} %weight_ref.1, s32[96,128]{1,0:T(8,128)} %valid_ref.1), custom_call_target="tpu_custom_call" | custom-call | tf_op jit(solution)/shard_map/block_terms/pallas_call | solution.py:194
  39.6 1.6 reshape.60
  41.2 4.4 %all-to-all-start.3 = ((f32[32,6,128]{2,1,0:T(8,128)}), f32[32,6,128]{2,1,0:T(8,128)S(1)}, u32[]{:S(2)}, u32[]{:S(2)}) async-start(f32[32,6,128]{2,1,0:T(8,128)} %reshape.60), calls=%async_computation.3 | async-start | bytes 262144 | tf_op jit(solution)/shard_map/all_to_all | solution.py:361
  45.6 0.1 convert_element_type.42
  45.7 0.0 copy-start.4
  45.7 1.2 copy.12
  46.9 4.7 %all-to-all-done.3 = f32[32,6,128]{2,1,0:T(8,128)S(1)} async-done(((f32[32,6,128]{2,1,0:T(8,128)}), f32[32,6,128]{2,1,0:T(8,128)S(1)}, u32[]{:S(2)}, u32[]{:S(2)}) %all-to-all-start.3) | async-done | bytes 98336 | tf_op jit(solution)/shard_map/all_to_all | solution.py:361
  51.5 5.0 %all-to-all-start = ((f16[1,4,4,16,2048]{4,3,1,0,2:T(8,128)(2,1)}), f16[1,4,4,16,2048]{4,3,1,0,2:T(8,128)(2,1)S(1)}, u32[]{:S(2)}, u32[]{:S(2)}) async-start(f16[1,4,4,16,2048]{4,3,1,0,2:T(8,128)(2,1)} %copy.12), calls=%async_computation | async-start | bytes 2097152 | tf_op jit(solution)/shard_map/all_to_all | solution.py:363
  56.5 2.9 %collective-permute-start = (bf16[2,16,2048]{2,1,0:T(8,128)(2,1)S(1)}, bf16[2,16,2048]{2,1,0:T(8,128)(2,1)S(1)}, u32[]{:S(2)}, u32[]{:S(2)}) collective-permute-start(bf16[2,16,2048]{2,1,0:T(8,128)(2,1)S(1)} %get-tuple-element.12), channel_id=1, source_target_pairs={{0,1},{1,2},{2,3},{3,4},{4,5},{5,6},{6,7},{8,9},{9,10},{10,11},{11... | collective-permute-start | bytes 393224 | tf_op jit(solution)/shard_map/ppermute | solution.py:333
  59.5 3.8 %collective-permute-start.1 = (bf16[2,16,2048]{2,1,0:T(8,128)(2,1)S(1)}, bf16[2,16,2048]{2,1,0:T(8,128)(2,1)S(1)}, u32[]{:S(2)}, u32[]{:S(2)}) collective-permute-start(bf16[2,16,2048]{2,1,0:T(8,128)(2,1)S(1)} %get-tuple-element.11), channel_id=1, source_target_pairs={{1,0},{2,1},{3,2},{4,3},{5,4},{6,5},{7,6},{9,8},{10,9},{11,10},{12... | collective-permute-start | bytes 393224 | tf_op jit(solution)/shard_map/ppermute | solution.py:334
  63.3 0.7 constant_dynamic-slice_fusion.2.held_ref
  64.0 0.7 reshape.61.recv_ref
  64.7 4.0 %spread_forcing_3.1.f_ref = f32[4,16,2048]{2,1,0:T(8,128)} custom-call(s32[768]{0:T(1024)} %reshape.56.ids_ref, f32[192,128]{1,0:T(8,128)} %reshape.61.recv_ref), custom_call_target="tpu_custom_call" | custom-call | tf_op jit(solution)/shard_map/spread_forcing_3/pallas_call | solution.py:263
  68.7 0.7 all-to-all-done
  69.3 0.2 fusion
  69.5 2.9 %collective-permute-start.2 = (f16[4,2,16,2048]{3,2,1,0:T(8,128)(2,1)S(1)}, f16[4,2,16,2048]{3,2,1,0:T(8,128)(2,1)S(1)}, u32[]{:S(2)}, u32[]{:S(2)}) collective-permute-start(f16[4,2,16,2048]{3,2,1,0:T(8,128)(2,1)S(1)} %get-tuple-element.10), channel_id=1, source_target_pairs={{0,1},{1,2},{2,3},{3,4},{4,5},{5,6},{6,7},{8,9},{9,10},{10,11},{11... | collective-permute-start | bytes 1572872 | tf_op jit(solution)/shard_map/ppermute | solution.py:333
  72.4 3.8 %collective-permute-start.3 = (f16[4,2,16,2048]{3,2,1,0:T(8,128)(2,1)S(1)}, f16[4,2,16,2048]{3,2,1,0:T(8,128)(2,1)S(1)}, u32[]{:S(2)}, u32[]{:S(2)}) collective-permute-start(f16[4,2,16,2048]{3,2,1,0:T(8,128)(2,1)S(1)} %get-tuple-element.9), channel_id=1, source_target_pairs={{1,0},{2,1},{3,2},{4,3},{5,4},{6,5},{7,6},{9,8},{10,9},{11,10},{12... | collective-permute-start | bytes 1572872 | tf_op jit(solution)/shard_map/ppermute | solution.py:334
  76.3 1.5 bitcast_convert_fusion.1.c_ref
  77.8 17.1 %collective-permute-done.2 = f16[4,2,16,2048]{3,2,1,0:T(8,128)(2,1)S(1)} collective-permute-done((f16[4,2,16,2048]{3,2,1,0:T(8,128)(2,1)S(1)}, f16[4,2,16,2048]{3,2,1,0:T(8,128)(2,1)S(1)}, u32[]{:S(2)}, u32[]{:S(2)}) %collective-permute-start.2) | collective-permute-done | bytes 524320 | tf_op jit(solution)/shard_map/ppermute | solution.py:333
  94.9 1.1 convert_element_type.45.cl_ref
  96.0 1.3 collective-permute-done.3
  97.3 1.1 convert_element_type.46.ch_ref
  98.4 0.7 copy-done.5
  99.0 0.6 copy-done.6
  99.7 3.1 %sweep_3.1.held_ref = bf16[4,16,2048]{2,1,0:T(8,128)(2,1)} custom-call(bf16[4,16,2048]{2,1,0:T(8,128)(2,1)} %constant_dynamic-slice_fusion.2.held_ref, bf16[2,16,2048]{2,1,0:T(8,128)(2,1)} %copy-done.5, bf16[2,16,2048]{2,1,0:T(8,128)(2,1)} %copy-done.6, f32[4,4,16,2048]{3,2,1,0:T(8,128)} %bitcast_convert_fusion.1.c_ref, ...), custom_call_target="tpu_custom_call" | custom-call | tf_op jit(solution)/shard_map/sweep_3/pallas_call | solution.py:314
  102.8 1.0 fusion.3
  103.8 3.1 %collective-permute-start.4 = (bf16[2,16,2048]{2,1,0:T(8,128)(2,1)S(1)}, bf16[2,16,2048]{2,1,0:T(8,128)(2,1)S(1)}, u32[]{:S(2)}, u32[]{:S(2)}) collective-permute-start(bf16[2,16,2048]{2,1,0:T(8,128)(2,1)S(1)} %get-tuple-element.18), channel_id=1, source_target_pairs={{0,1},{1,2},{2,3},{3,4},{4,5},{5,6},{6,7},{8,9},{9,10},{10,11},{11... | collective-permute-start | bytes 393224 | tf_op jit(solution)/shard_map/ppermute | solution.py:333
  106.8 3.7 %collective-permute-start.5 = (bf16[2,16,2048]{2,1,0:T(8,128)(2,1)S(1)}, bf16[2,16,2048]{2,1,0:T(8,128)(2,1)S(1)}, u32[]{:S(2)}, u32[]{:S(2)}) collective-permute-start(bf16[2,16,2048]{2,1,0:T(8,128)(2,1)S(1)} %get-tuple-element.17), channel_id=1, source_target_pairs={{1,0},{2,1},{3,2},{4,3},{5,4},{6,5},{7,6},{9,8},{10,9},{11,10},{12... | collective-permute-start | bytes 393224 | tf_op jit(solution)/shard_map/ppermute | solution.py:334
  110.5 4.0 %spread_forcing_2.1.f_ref = f32[4,16,2048]{2,1,0:T(8,128)} custom-call(s32[768]{0:T(1024)} %reshape.56.ids_ref, f32[192,128]{1,0:T(8,128)} %reshape.61.recv_ref), custom_call_target="tpu_custom_call" | custom-call | tf_op jit(solution)/shard_map/spread_forcing_2/pallas_call | solution.py:263
  114.5 0.3 collective-permute-done.5.high_ref
  114.8 0.4 copy-done.9
  115.2 0.6 copy-done.11
  115.8 3.1 %sweep_2.1.held_ref = bf16[4,16,2048]{2,1,0:T(8,128)(2,1)} custom-call(bf16[4,16,2048]{2,1,0:T(8,128)(2,1)} %sweep_3.1.held_ref, bf16[2,16,2048]{2,1,0:T(8,128)(2,1)} %copy-done.9, bf16[2,16,2048]{2,1,0:T(8,128)(2,1)} %copy-done.11, f32[4,4,16,2048]{3,2,1,0:T(8,128)} %bitcast_convert_fusion.1.c_ref, f32[4,2,16,2048]{3,2,1,0:T(8,128)} %convert_element_type.45.cl_ref, ...), custom_call_target="tpu_custom_call" | custom-call | tf_op jit(solution)/shard_map/sweep_2/pallas_call | solution.py:314
  118.9 1.0 fusion.2
  119.9 2.8 %collective-permute-start.6 = (bf16[2,16,2048]{2,1,0:T(8,128)(2,1)S(1)}, bf16[2,16,2048]{2,1,0:T(8,128)(2,1)S(1)}, u32[]{:S(2)}, u32[]{:S(2)}) collective-permute-start(bf16[2,16,2048]{2,1,0:T(8,128)(2,1)S(1)} %get-tuple-element.16), channel_id=1, source_target_pairs={{0,1},{1,2},{2,3},{3,4},{4,5},{5,6},{6,7},{8,9},{9,10},{10,11},{11... | collective-permute-start | bytes 393224 | tf_op jit(solution)/shard_map/ppermute | solution.py:333
  122.7 3.9 %collective-permute-start.7 = (bf16[2,16,2048]{2,1,0:T(8,128)(2,1)S(1)}, bf16[2,16,2048]{2,1,0:T(8,128)(2,1)S(1)}, u32[]{:S(2)}, u32[]{:S(2)}) collective-permute-start(bf16[2,16,2048]{2,1,0:T(8,128)(2,1)S(1)} %get-tuple-element.15), channel_id=1, source_target_pairs={{1,0},{2,1},{3,2},{4,3},{5,4},{6,5},{7,6},{9,8},{10,9},{11,10},{12... | collective-permute-start | bytes 393224 | tf_op jit(solution)/shard_map/ppermute | solution.py:334
  126.7 4.0 %spread_forcing_1.1.f_ref = f32[4,16,2048]{2,1,0:T(8,128)} custom-call(s32[768]{0:T(1024)} %reshape.56.ids_ref, f32[192,128]{1,0:T(8,128)} %reshape.61.recv_ref), custom_call_target="tpu_custom_call" | custom-call | tf_op jit(solution)/shard_map/spread_forcing_1/pallas_call | solution.py:263
  130.7 0.0 collective-permute-done.6.low_ref
  130.7 0.0 collective-permute-done.7.high_ref
  130.7 0.6 copy-done.10
  131.3 0.7 copy-done.12
  132.0 3.1 %sweep_1.1.held_ref = bf16[4,16,2048]{2,1,0:T(8,128)(2,1)} custom-call(bf16[4,16,2048]{2,1,0:T(8,128)(2,1)} %sweep_2.1.held_ref, bf16[2,16,2048]{2,1,0:T(8,128)(2,1)} %copy-done.10, bf16[2,16,2048]{2,1,0:T(8,128)(2,1)} %copy-done.12, f32[4,4,16,2048]{3,2,1,0:T(8,128)} %bitcast_convert_fusion.1.c_ref, f32[4,2,16,2048]{3,2,1,0:T(8,128)} %convert_element_type.45.cl_ref, ...), custom_call_target="tpu_custom_call" | custom-call | tf_op jit(solution)/shard_map/sweep_1/pallas_call | solution.py:314
  135.0 1.0 fusion.1
  136.0 2.7 %collective-permute-start.8 = (bf16[2,16,2048]{2,1,0:T(8,128)(2,1)S(1)}, bf16[2,16,2048]{2,1,0:T(8,128)(2,1)S(1)}, u32[]{:S(2)}, u32[]{:S(2)}) collective-permute-start(bf16[2,16,2048]{2,1,0:T(8,128)(2,1)S(1)} %get-tuple-element.14), channel_id=1, source_target_pairs={{0,1},{1,2},{2,3},{3,4},{4,5},{5,6},{6,7},{8,9},{9,10},{10,11},{11... | collective-permute-start | bytes 393224 | tf_op jit(solution)/shard_map/ppermute | solution.py:333
  138.7 4.1 %collective-permute-start.9 = (bf16[2,16,2048]{2,1,0:T(8,128)(2,1)S(1)}, bf16[2,16,2048]{2,1,0:T(8,128)(2,1)S(1)}, u32[]{:S(2)}, u32[]{:S(2)}) collective-permute-start(bf16[2,16,2048]{2,1,0:T(8,128)(2,1)S(1)} %get-tuple-element.13), channel_id=1, source_target_pairs={{1,0},{2,1},{3,2},{4,3},{5,4},{6,5},{7,6},{9,8},{10,9},{11,10},{12... | collective-permute-start | bytes 393224 | tf_op jit(solution)/shard_map/ppermute | solution.py:334
  142.8 4.0 %spread_forcing_0.1.f_ref = f32[4,16,2048]{2,1,0:T(8,128)} custom-call(s32[768]{0:T(1024)} %reshape.56.ids_ref, f32[192,128]{1,0:T(8,128)} %reshape.61.recv_ref), custom_call_target="tpu_custom_call" | custom-call | tf_op jit(solution)/shard_map/spread_forcing_0/pallas_call | solution.py:263
  146.8 0.0 collective-permute-done.9.high_ref
  146.8 0.6 copy-done.7
  147.4 0.6 copy-done.8
  148.1 3.1 %sweep_0.1 = bf16[4,16,2048]{2,1,0:T(8,128)(2,1)} custom-call(bf16[4,16,2048]{2,1,0:T(8,128)(2,1)} %sweep_1.1.held_ref, bf16[2,16,2048]{2,1,0:T(8,128)(2,1)} %copy-done.7, bf16[2,16,2048]{2,1,0:T(8,128)(2,1)} %copy-done.8, f32[4,4,16,2048]{3,2,1,0:T(8,128)} %bitcast_convert_fusion.1.c_ref, f32[4,2,16,2048]{3,2,1,0:T(8,128)} %convert_element_type.45.cl_ref, ...), custom_call_target="tpu_custom_call" | custom-call | tf_op jit(solution)/shard_map/sweep_0/pallas_call | solution.py:314
  151.2 1.1 maximum_bitcast_fusion
  152.3 16.5 %all_to_all.44 = bf16[4,4,1,16,2048]{4,3,1,2,0:T(8,128)(2,1)S(1)} all-to-all(bf16[4,4,1,16,2048]{4,3,1,2,0:T(8,128)(2,1)S(1)} %maximum_bitcast_fusion), channel_id=1, replica_groups=mesh['tm'=4,'lat'=8] {'tm'}, dimensions={0} | all-to-all | bytes 2097152 | tf_op jit(solution)/shard_map/all_to_all | solution.py:387
  168.8 1.6 bitcast_convert_fusion
  (22 shorter events, 0.1 us)
Async XLA Ops:
  4.5 11.0 %all-to-all-start.1 = ((s32[32,1,24]{2,1,0:T(1,128)}), s32[32,1,24]{2,1,0:T(1,128)S(1)}, u32[]{:S(2)}, u32[]{:S(2)}) async-start(s32[32,1,24]{2,1,0:T(1,128)} %bitcast.7), calls=%async_computation.1 | async-start | bytes 32768 | tf_op jit(solution)/shard_map/all_to_all | solution.py:361
  33.4 12.1 %copy-start.3 = (f32[1,4,64,2048]{3,2,1,0:T(8,128)S(1)}, f32[1,4,64,2048]{3,2,1,0:T(8,128)}, u32[]{:S(2)}) copy-start(f32[1,4,64,2048]{3,2,1,0:T(8,128)} %param.10) | copy-start | bytes 6291460
  41.2 10.4 %all-to-all-start.3 = ((f32[32,6,128]{2,1,0:T(8,128)}), f32[32,6,128]{2,1,0:T(8,128)S(1)}, u32[]{:S(2)}, u32[]{:S(2)}) async-start(f32[32,6,128]{2,1,0:T(8,128)} %reshape.60), calls=%async_computation.3 | async-start | bytes 262144 | tf_op jit(solution)/shard_map/all_to_all | solution.py:361
  45.7 10.8 %copy-start.4 = (bf16[4,64,2048]{2,1,0:T(8,128)(2,1)S(1)}, bf16[4,64,2048]{2,1,0:T(8,128)(2,1)}, u32[]{:S(2)}) copy-start(bf16[4,64,2048]{2,1,0:T(8,128)(2,1)} %param.11) | copy-start | bytes 3145732
  51.5 17.8 %all-to-all-start = ((f16[1,4,4,16,2048]{4,3,1,0,2:T(8,128)(2,1)}), f16[1,4,4,16,2048]{4,3,1,0,2:T(8,128)(2,1)S(1)}, u32[]{:S(2)}, u32[]{:S(2)}) async-start(f16[1,4,4,16,2048]{4,3,1,0,2:T(8,128)(2,1)} %copy.12), calls=%async_computation | async-start | bytes 2097152 | tf_op jit(solution)/shard_map/all_to_all | solution.py:363
  56.5 41.8 %collective-permute-start = (bf16[2,16,2048]{2,1,0:T(8,128)(2,1)S(1)}, bf16[2,16,2048]{2,1,0:T(8,128)(2,1)S(1)}, u32[]{:S(2)}, u32[]{:S(2)}) collective-permute-start(bf16[2,16,2048]{2,1,0:T(8,128)(2,1)S(1)} %get-tuple-element.12), channel_id=1, source_target_pairs={{0,1},{1,2},{2,3},{3,4},{4,5},{5,6},{6,7},{8,9},{9,10},{10,11},{11... | collective-permute-start | bytes 393224 | tf_op jit(solution)/shard_map/ppermute | solution.py:333
  59.5 38.9 %collective-permute-start.1 = (bf16[2,16,2048]{2,1,0:T(8,128)(2,1)S(1)}, bf16[2,16,2048]{2,1,0:T(8,128)(2,1)S(1)}, u32[]{:S(2)}, u32[]{:S(2)}) collective-permute-start(bf16[2,16,2048]{2,1,0:T(8,128)(2,1)S(1)} %get-tuple-element.11), channel_id=1, source_target_pairs={{1,0},{2,1},{3,2},{4,3},{5,4},{6,5},{7,6},{9,8},{10,9},{11,10},{12... | collective-permute-start | bytes 393224 | tf_op jit(solution)/shard_map/ppermute | solution.py:334
  69.5 25.4 %collective-permute-start.2 = (f16[4,2,16,2048]{3,2,1,0:T(8,128)(2,1)S(1)}, f16[4,2,16,2048]{3,2,1,0:T(8,128)(2,1)S(1)}, u32[]{:S(2)}, u32[]{:S(2)}) collective-permute-start(f16[4,2,16,2048]{3,2,1,0:T(8,128)(2,1)S(1)} %get-tuple-element.10), channel_id=1, source_target_pairs={{0,1},{1,2},{2,3},{3,4},{4,5},{5,6},{6,7},{8,9},{9,10},{10,11},{11... | collective-permute-start | bytes 1572872 | tf_op jit(solution)/shard_map/ppermute | solution.py:333
  72.4 24.9 %collective-permute-start.3 = (f16[4,2,16,2048]{3,2,1,0:T(8,128)(2,1)S(1)}, f16[4,2,16,2048]{3,2,1,0:T(8,128)(2,1)S(1)}, u32[]{:S(2)}, u32[]{:S(2)}) collective-permute-start(f16[4,2,16,2048]{3,2,1,0:T(8,128)(2,1)S(1)} %get-tuple-element.9), channel_id=1, source_target_pairs={{1,0},{2,1},{3,2},{4,3},{5,4},{6,5},{7,6},{9,8},{10,9},{11,10},{12... | collective-permute-start | bytes 1572872 | tf_op jit(solution)/shard_map/ppermute | solution.py:334
  98.4 0.7 copy-start.5
  99.0 0.6 copy-start.6
  103.8 10.7 %collective-permute-start.4 = (bf16[2,16,2048]{2,1,0:T(8,128)(2,1)S(1)}, bf16[2,16,2048]{2,1,0:T(8,128)(2,1)S(1)}, u32[]{:S(2)}, u32[]{:S(2)}) collective-permute-start(bf16[2,16,2048]{2,1,0:T(8,128)(2,1)S(1)} %get-tuple-element.18), channel_id=1, source_target_pairs={{0,1},{1,2},{2,3},{3,4},{4,5},{5,6},{6,7},{8,9},{9,10},{10,11},{11... | collective-permute-start | bytes 393224 | tf_op jit(solution)/shard_map/ppermute | solution.py:333
  106.8 8.0 %collective-permute-start.5 = (bf16[2,16,2048]{2,1,0:T(8,128)(2,1)S(1)}, bf16[2,16,2048]{2,1,0:T(8,128)(2,1)S(1)}, u32[]{:S(2)}, u32[]{:S(2)}) collective-permute-start(bf16[2,16,2048]{2,1,0:T(8,128)(2,1)S(1)} %get-tuple-element.17), channel_id=1, source_target_pairs={{1,0},{2,1},{3,2},{4,3},{5,4},{6,5},{7,6},{9,8},{10,9},{11,10},{12... | collective-permute-start | bytes 393224 | tf_op jit(solution)/shard_map/ppermute | solution.py:334
  114.5 0.7 copy-start.9
  115.2 0.6 copy-start.11
  119.9 10.7 %collective-permute-start.6 = (bf16[2,16,2048]{2,1,0:T(8,128)(2,1)S(1)}, bf16[2,16,2048]{2,1,0:T(8,128)(2,1)S(1)}, u32[]{:S(2)}, u32[]{:S(2)}) collective-permute-start(bf16[2,16,2048]{2,1,0:T(8,128)(2,1)S(1)} %get-tuple-element.16), channel_id=1, source_target_pairs={{0,1},{1,2},{2,3},{3,4},{4,5},{5,6},{6,7},{8,9},{9,10},{10,11},{11... | collective-permute-start | bytes 393224 | tf_op jit(solution)/shard_map/ppermute | solution.py:333
  122.7 7.9 %collective-permute-start.7 = (bf16[2,16,2048]{2,1,0:T(8,128)(2,1)S(1)}, bf16[2,16,2048]{2,1,0:T(8,128)(2,1)S(1)}, u32[]{:S(2)}, u32[]{:S(2)}) collective-permute-start(bf16[2,16,2048]{2,1,0:T(8,128)(2,1)S(1)} %get-tuple-element.15), channel_id=1, source_target_pairs={{1,0},{2,1},{3,2},{4,3},{5,4},{6,5},{7,6},{9,8},{10,9},{11,10},{12... | collective-permute-start | bytes 393224 | tf_op jit(solution)/shard_map/ppermute | solution.py:334
  130.7 0.6 copy-start.10
  131.3 0.7 copy-start.12
  136.0 10.8 %collective-permute-start.8 = (bf16[2,16,2048]{2,1,0:T(8,128)(2,1)S(1)}, bf16[2,16,2048]{2,1,0:T(8,128)(2,1)S(1)}, u32[]{:S(2)}, u32[]{:S(2)}) collective-permute-start(bf16[2,16,2048]{2,1,0:T(8,128)(2,1)S(1)} %get-tuple-element.14), channel_id=1, source_target_pairs={{0,1},{1,2},{2,3},{3,4},{4,5},{5,6},{6,7},{8,9},{9,10},{10,11},{11... | collective-permute-start | bytes 393224 | tf_op jit(solution)/shard_map/ppermute | solution.py:333
  138.7 8.1 %collective-permute-start.9 = (bf16[2,16,2048]{2,1,0:T(8,128)(2,1)S(1)}, bf16[2,16,2048]{2,1,0:T(8,128)(2,1)S(1)}, u32[]{:S(2)}, u32[]{:S(2)}) collective-permute-start(bf16[2,16,2048]{2,1,0:T(8,128)(2,1)S(1)} %get-tuple-element.13), channel_id=1, source_target_pairs={{1,0},{2,1},{3,2},{4,3},{5,4},{6,5},{7,6},{9,8},{10,9},{11,10},{12... | collective-permute-start | bytes 393224 | tf_op jit(solution)/shard_map/ppermute | solution.py:334
  146.8 4.4 %copy-start = (bf16[4,16,2048]{2,1,0:T(8,128)(2,1)S(1)}, bf16[4,16,2048]{2,1,0:T(8,128)(2,1)}, u32[]{:S(2)}) copy-start(bf16[4,16,2048]{2,1,0:T(8,128)(2,1)} %sweep_3.1.held_ref) | copy-start | bytes 786436
  146.8 4.4 %copy-start.1 = (bf16[4,16,2048]{2,1,0:T(8,128)(2,1)S(1)}, bf16[4,16,2048]{2,1,0:T(8,128)(2,1)}, u32[]{:S(2)}) copy-start(bf16[4,16,2048]{2,1,0:T(8,128)(2,1)} %sweep_2.1.held_ref) | copy-start | bytes 786436
  146.8 4.4 %copy-start.2 = (bf16[4,16,2048]{2,1,0:T(8,128)(2,1)S(1)}, bf16[4,16,2048]{2,1,0:T(8,128)(2,1)}, u32[]{:S(2)}) copy-start(bf16[4,16,2048]{2,1,0:T(8,128)(2,1)} %sweep_1.1.held_ref) | copy-start | bytes 786436
  146.8 0.7 copy-start.7
  147.4 0.6 copy-start.8
